TPU v7x, 32 devices: a whole 2x2x4 slice. The times are simulated.
32 devices in a mesh: dp: 8 (over y, x, core), seq: 4 (over z).
Axes of the slice: x: 2, y: 2, z: 4, core: 2. Of those that a mesh axis runs over, the one named last changes fastest.
Arguments:
- tokens: bfloat16 [8, 512, 1024], P('dp', 'seq'), may hold values from -6 to 6
- cotangent: bfloat16 [8, 512, 1024], P('dp', 'seq'), may hold values from -6 to 6
- stamps: int32 [8, 512], P('dp'), may hold values from 0 to 1080832, as said below
- lengths: int32 [8], P('dp'), may hold values from 64 to 512, as said below
- w_qkvu: bfloat16 [1024, 4096], P('dp'), may hold values from -0.1875 to 0.1875
- w_out: bfloat16 [1024, 1024], P('dp'), may hold values from -0.1875 to 0.1875
- gain_in: float32 [1024], replicated, may hold values from 0.25 to 1.75
- gain_out: float32 [1024], replicated, may hold values from 0.25 to 1.75
- bias_table: float32 [8, 16], replicated, may hold values from -4 to 4
Outputs:
- mixed: bfloat16 [8, 512, 1024], P('dp', 'seq')
- input_grad: bfloat16 [8, 512, 1024], P('dp', 'seq')
- out_weight_grad: float32 [1024, 1024], P('dp')
Inputs may be any that keep to these rules, and one draw needn't show every extreme that they name: `lengths`: each stream has 64 valid actions or more; some stream is full. `stamps`: timestamps never fall along a stream, and consecutive ones differ by less than 64.
All inputs are finite; a program needn't handle non-finite values.
Results may differ from a plain program's by a relative error of at most 0.019.
Values may be sent and summed in bfloat16 or wider, within the bound.
A program may use at most 128 MiB of HBM per device.

v0:
```python
import jax
import jax.numpy as jnp
from jax import lax
from jax.sharding import PartitionSpec as P

H = 8
DH = 128


EPS = 1e-05


def layer_norm(values, gain):
    average = jnp.mean(values, axis=-1, keepdims=True)
    centred = values - average
    variance = jnp.mean(centred * centred, axis=-1, keepdims=True)
    return centred * lax.rsqrt(variance + EPS) * gain


def silu_slope(values):
    sigmoid_v = jax.nn.sigmoid(values)
    return sigmoid_v * (1.0 + values * (1.0 - sigmoid_v))


def time_bias(bias_table, stamps_q, stamps_k):
    elapsed = stamps_q[:, None] - stamps_k[None, :]
    bucket = jnp.zeros(elapsed.shape, jnp.int32)
    for degree in range(1, bias_table.shape[1]):
        bucket = bucket + (elapsed >= 2**degree - 1).astype(jnp.int32)
    levels = jnp.arange(bias_table.shape[1], dtype=jnp.int32)
    one_hot = (bucket[:, :, None] == levels[None, None, :]).astype(jnp.float32)
    return jnp.einsum(
        "qkb,hb->hqk",
        one_hot,
        bias_table,
        precision=lax.Precision.HIGHEST,
        preferred_element_type=jnp.float32,
    )


def pair_terms(
    q_heads, d_heads, stamps_q, pos_q, k_heads, v_heads, stamps_k, pos_k, length, bias_table, scale
):
    scores = (
        jnp.einsum("qhd,khd->hqk", q_heads, k_heads, preferred_element_type=jnp.float32) * scale
    )
    scores = scores + time_bias(bias_table, stamps_q, stamps_k)
    allowed = (
        (pos_k[None, :] <= pos_q[:, None]) & (pos_k[None, :] < length) & (pos_q[:, None] < length)
    )
    weight = jnp.where(allowed[None], jax.nn.silu(scores), 0.0).astype(jnp.bfloat16)
    if d_heads is None:
        return (weight, None)
    d_weight = jnp.einsum("qhd,khd->hqk", d_heads, v_heads, preferred_element_type=jnp.float32)
    d_scores = jnp.where(allowed[None], d_weight * silu_slope(scores), 0.0).astype(jnp.bfloat16)
    return (weight, d_scores)


def per_device(tokens, cotangent, stamps, lengths, w_qkvu, w_out, gain_in, gain_out, bias_table):
    rows = tokens[0]
    cot_rows = cotangent[0]
    tok_count = rows.shape[0]
    feature_width = rows.shape[1]
    seq_count = lax.axis_size("seq")
    total_rows = tok_count * seq_count
    first_row = lax.axis_index("seq") * tok_count
    length = lengths[0]
    stamp_all = stamps[0]
    pos_own = first_row + jnp.arange(tok_count, dtype=jnp.int32)
    stamp_own = lax.dynamic_slice_in_dim(stamp_all, first_row, tok_count)
    scale = DH ** (-0.5)
    block_rows = min(512, total_rows)
    block_count = total_rows // block_rows
    w_full, w_out_full = (
        lax.all_gather(w_qkvu, "dp", axis=0, tiled=True),
        lax.all_gather(w_out, "dp", axis=0, tiled=True),
    )
    wide_rows = rows.astype(jnp.float32)
    normed = layer_norm(wide_rows, gain_in).astype(jnp.bfloat16)
    projected = jnp.dot(normed, w_full, preferred_element_type=jnp.float32)
    activated = jax.nn.silu(projected)
    gate_u = activated[:, :feature_width]
    values_own = activated[:, feature_width : 2 * feature_width].astype(jnp.bfloat16)
    queries_own = activated[:, 2 * feature_width : 3 * feature_width].astype(jnp.bfloat16)
    keys_own = activated[:, 3 * feature_width :].astype(jnp.bfloat16)
    keys_all, values_all = (
        lax.all_gather(keys_own, "seq", axis=0, tiled=True),
        lax.all_gather(values_own, "seq", axis=0, tiled=True),
    )
    q_heads = queries_own.reshape(tok_count, H, DH)

    def key_block(start):
        k_heads = lax.dynamic_slice_in_dim(keys_all, start, block_rows).reshape(block_rows, H, DH)
        v_heads = lax.dynamic_slice_in_dim(values_all, start, block_rows).reshape(block_rows, H, DH)
        stamps_k = lax.dynamic_slice_in_dim(stamp_all, start, block_rows)
        pos_k = start + jnp.arange(block_rows, dtype=jnp.int32)
        return (k_heads, v_heads, stamps_k, pos_k)

    def guarded(active, action, state):
        return lax.cond(active, action, lambda same: same, state)

    def reaches(start):
        return (start <= first_row + tok_count - 1) & (start < length) & (first_row < length)

    def forward_step(block_idx, totals):
        start = block_idx * block_rows

        def forward_compute(totals):
            k_heads, v_heads, stamps_k, pos_k = key_block(start)
            weight, unused = pair_terms(
                q_heads,
                None,
                stamp_own,
                pos_own,
                k_heads,
                v_heads,
                stamps_k,
                pos_k,
                length,
                bias_table,
                scale,
            )
            return totals + jnp.einsum(
                "hqk,khd->qhd", weight, v_heads, preferred_element_type=jnp.float32
            )

        return guarded(reaches(start), forward_compute, totals)

    attended = lax.fori_loop(
        0, block_count, forward_step, jnp.zeros((tok_count, H, DH), jnp.float32)
    )
    attended = attended.reshape(tok_count, feature_width)
    normed_att, norm_back = jax.vjp(lambda values: layer_norm(values, gain_out), attended)
    mixed_rows = (normed_att * gate_u).astype(jnp.bfloat16)
    mixed = (
        wide_rows + jnp.dot(mixed_rows, w_out_full, preferred_element_type=jnp.float32)
    ).astype(jnp.bfloat16)
    grad_part = lax.psum_scatter(
        jnp.einsum("tr,tc->rc", mixed_rows, cot_rows, preferred_element_type=jnp.float32).astype(
            jnp.bfloat16
        ),
        "dp",
        scatter_dimension=0,
        tiled=True,
    )
    w_grad = lax.psum(grad_part, "seq").astype(jnp.float32)
    d_mix = jnp.einsum("tc,rc->tr", cot_rows, w_out_full, preferred_element_type=jnp.float32)
    d_gate = d_mix * normed_att
    d_att = norm_back(d_mix * gate_u)[0].astype(jnp.bfloat16)
    d_heads = d_att.reshape(tok_count, H, DH)

    def backward_step():

        def step(block_idx, state_pair):
            start = block_idx * block_rows

            def step_compute(state_pair):
                q_grad, key_terms = state_pair
                k_heads, v_heads, stamps_k, pos_k = key_block(start)
                weight, d_scores = pair_terms(
                    q_heads,
                    d_heads,
                    stamp_own,
                    pos_own,
                    k_heads,
                    v_heads,
                    stamps_k,
                    pos_k,
                    length,
                    bias_table,
                    scale,
                )
                q_grad = (
                    q_grad
                    + jnp.einsum(
                        "hqk,khd->qhd", d_scores, k_heads, preferred_element_type=jnp.float32
                    )
                    * scale
                )
                k_grad = (
                    jnp.einsum(
                        "hqk,qhd->khd", d_scores, q_heads, preferred_element_type=jnp.float32
                    )
                    * scale
                )
                v_grad = jnp.einsum(
                    "hqk,qhd->khd", weight, d_heads, preferred_element_type=jnp.float32
                )
                joined = jnp.concatenate(
                    [
                        k_grad.reshape(block_rows, feature_width),
                        v_grad.reshape(block_rows, feature_width),
                    ],
                    axis=1,
                )
                key_terms = lax.dynamic_update_slice_in_dim(key_terms, joined, start, 0)
                return (q_grad, key_terms)

            return guarded(reaches(start), step_compute, state_pair)

        return step

    q_start = jnp.zeros((tok_count, H, DH), jnp.float32)
    term_start = jnp.zeros((total_rows, 2 * feature_width), jnp.float32)
    q_grad, key_terms = lax.fori_loop(0, block_count, backward_step(), (q_start, term_start))
    key_grads = lax.psum_scatter(
        key_terms.astype(jnp.bfloat16), "seq", scatter_dimension=0, tiled=True
    ).astype(jnp.float32)
    d_act = jnp.concatenate(
        [
            d_gate,
            key_grads[:, feature_width:],
            q_grad.reshape(tok_count, feature_width),
            key_grads[:, :feature_width],
        ],
        axis=1,
    )
    d_proj = (d_act * silu_slope(projected)).astype(jnp.bfloat16)
    d_normed = jnp.einsum("tf,df->td", d_proj, w_full, preferred_element_type=jnp.float32)
    unused_rows, in_back = jax.vjp(lambda values: layer_norm(values, gain_in), wide_rows)
    input_grad = (cot_rows.astype(jnp.float32) + in_back(d_normed)[0]).astype(jnp.bfloat16)
    return (mixed[None], input_grad[None], w_grad)


def solution(mesh):
    return jax.shard_map(
        per_device,
        mesh=mesh,
        in_specs=(
            P("dp", "seq", None),
            P("dp", "seq", None),
            P("dp", None),
            P("dp"),
            P("dp", None),
            P("dp", None),
            P(),
            P(),
            P(),
        ),
        out_specs=(P("dp", "seq", None), P("dp", "seq", None), P("dp", None)),
        check_vma=False,
    )
```

profile of v0, /device:TPU:3, one launch (start us, length us, event | category | flops | bytes accessed | tf_op | source)
XLA Modules:
  0.0 307.5 jit_solution(9463237109078155337)
XLA Ops:
  7.9 1.1 convert_reduce_fusion
  9.0 1.2 fusion.49
  10.2 55.6 %all-gather.5.cloned.1.call-done = bf16[1024,4096]{1,0:T(8,128)(2,1)} async-done(((bf16[128,4096]{1,0:T(8,128)(2,1)}), bf16[1024,4096]{1,0:T(8,128)(2,1)}) %all-gather.5.cloned.1.call-update) | async-done | bytes 8388624 | tf_op jit(solution)/shard_map/all_gather | solution.py:75
  65.8 7.0 %fusion.69 = (bf16[128,4096]{1,0:T(8,128)(2,1)S(1)}, f32[128,4096]{1,0:T(8,128)}, f32[128,4096]{1,0:T(8,128)}) fusion(bf16[1024,4096]{1,0:T(8,128)(2,1)} %all-gather.5.cloned.1.call-done, bf16[1,128,1024]{2,1,0:T(8,128)(2,1)} %param.13, f32[1024]{0:T(1024)} %param.19, f32[128]{0:T(128)S(1)} %fusion.63, f32[128]{0:T(128)S(1)} %broadcast_multiply_fusion.1), kind=kOutput, calls=%fused_computation.143 | convolution fusion | flops 1077018624 | bytes 13898752 | tf_op jit(solution)/shard_map/dot_general | solution.py:80
  72.8 0.9 fusion.71
  75.8 25.1 %all-gather.7.cloned.1.call-done = bf16[512,1024]{1,0:T(8,128)(2,1)} async-done(((bf16[128,1024]{1,0:T(8,128)(2,1)}), bf16[512,1024]{1,0:T(8,128)(2,1)}) %all-gather.7.cloned.1.call-update) | async-done | bytes 1048592 | tf_op jit(solution)/shard_map/all_gather | solution.py:87
  100.9 29.5 %all-gather.9.cloned.1.call-done = bf16[512,1024]{1,0:T(8,128)(2,1)} async-done(((bf16[128,1024]{1,0:T(8,128)(2,1)}), bf16[512,1024]{1,0:T(8,128)(2,1)}) %all-gather.9.cloned.1.call-update) | async-done | bytes 1048592 | tf_op jit(solution)/shard_map/all_gather | solution.py:88
  130.5 8.8 %conditional.2 = (f32[128,8,128]{2,0,1:T(8,128)S(1)}) conditional(s32[]{:T(128)} %convert_element_type.288, f32[128,8,128]{2,0,1:T(8,128)S(1)} %broadcast.484, (s32[128]{0:T(128)S(1)}, s32[]{:T(128)}, bf16[512,1024]{1,0:T(8,128)(2,1)}, bf16[128,8,128]{2,1,0:T(8,128)(2,1)S(1)}, s32[128]{0:T(128)S(1)}, /*index=5*/s32[512]{0:T(512)S(1)}, ...), branch_computations={%region_2.3_spmd, %region_3.0_spmd} | conditional | flops 377619072 | bytes 12457260 | solution.py:100
  131.0 2.7 fusion
  135.2 4.2 %fusion.2 = f32[128,8,128]{2,0,1:T(8,128)S(1)} fusion(f32[128,8,128]{2,0,1:T(8,128)S(1)} %get-tuple-element.155, f32[128,512,8]{1,2,0:T(8,128)} %fusion, pred[128,512]{1,0:T(8,128)(4,1)S(1)} %fusion.16, bf16[128,8,128]{2,1,0:T(8,128)(2,1)S(1)} %get-tuple-element.184, bf16[512,1024]{1,0:T(8,128)(2,1)} %get-tuple-element.163, bf16[512,1024]{1,0:T(8,128)(2,1)S(1)} %copy-done.2), kind=kOutput, calls=%fused_computation.21 | convolution fusion | flops 272760832 | bytes 5570560 | tf_op jit(solution)/shard_map/while/body/eval_jaxpr/cond/branch_1_fun/hqk,khd->qhd/dot_general | solution.py:123
  139.7 20.6 %all-gather.11.cloned.1.call-done = bf16[1024,1024]{1,0:T(8,128)(2,1)} async-done(((bf16[128,1024]{1,0:T(8,128)(2,1)}), bf16[1024,1024]{1,0:T(8,128)(2,1)}) %all-gather.11.cloned.1.call-update) | async-done | bytes 2097168 | tf_op jit(solution)/shard_map/all_gather | solution.py:76
  160.3 2.6 multiply_reduce_fusion
  162.9 2.1 fusion.68
  165.1 2.0 convolution_convert_fusion
  167.2 40.6 %reduce-scatter.5.cloned.1.call-done = bf16[128,1024]{1,0:T(8,128)(2,1)} async-done(((bf16[1024,1024]{1,0:T(8,128)(2,1)}), bf16[128,1024]{1,0:T(8,128)(2,1)}) %reduce-scatter.5.cloned.1.call-update) | async-done | bytes 262160 | tf_op jit(solution)/shard_map/reduce_scatter | solution.py:138
  208.0 13.3 %conditional.3 = (bf16[512,2048]{0,1:T(8,128)(2,1)}, f32[128,8,128]{2,0,1:T(8,128)S(1)}) conditional(s32[]{:T(128)} %convert_element_type.288, f32[128,8,128]{2,0,1:T(8,128)S(1)} %broadcast.484, (s32[128]{0:T(128)S(1)}, s32[]{:T(128)}, bf16[128,1024]{1,0:T(8,128)(2,1)S(1)}, bf16[512,1024]{1,0:T(8,128)(2,1)}, bf16[512,1024]{1,0:T(8,128)(2,1)}, ...), branch_computations={%region_8.9_spmd, %region_9.10_spmd} | conditional | flops 790889088 | bytes 37426568 | solution.py:100
  208.2 0.8 copy.23
  209.5 1.3 fusion.21
  210.9 1.2 copy.24
  212.0 2.8 bitcast_add_fusion.1
  216.3 0.9 fusion.29
  217.5 1.1 select_convert_fusion.2
  219.1 1.4 pad_maximum_fusion
  221.3 4.0 %copy.25 = bf16[512,2048]{1,0:T(8,128)(2,1)} copy(bf16[512,2048]{0,1:T(8,128)(2,1)} %get-tuple-element.179) | data formatting | bytes 4194304 | tf_op jit(solution)/shard_map/while/body/eval_jaxpr/cond | solution.py:100
  225.4 1.6 copy-done
  226.9 1.2 fusion.41
  228.1 15.8 %all-reduce.2.cloned.1.call-done = bf16[128,1024]{1,0:T(8,128)(2,1)} async-done(((bf16[128,1024]{1,0:T(8,128)(2,1)}), bf16[128,1024]{1,0:T(8,128)(2,1)}) %all-reduce.2.cloned.1.call-update) | async-done | bytes 262160 | tf_op jit(solution)/shard_map/psum | solution.py:146
  243.9 1.8 convert_element_type.299
  245.7 45.5 %reduce-scatter.3.cloned.1.call-done = bf16[128,2048]{1,0:T(8,128)(2,1)} async-done(((bf16[512,2048]{1,0:T(8,128)(2,1)}), bf16[128,2048]{1,0:T(8,128)(2,1)}) %reduce-scatter.3.cloned.1.call-update) | async-done | bytes 524304 | tf_op jit(solution)/shard_map/reduce_scatter | solution.py:206
  291.2 1.3 fusion.72
  293.0 6.4 %fusion.52 = (f32[128]{0:T(128)S(1)}, f32[128,1024]{1,0:T(8,128)S(1)}) fusion(bf16[1,128,1024]{2,1,0:T(8,128)(2,1)S(1)} %copy-done.1, f32[128]{0:T(128)S(1)} %broadcast_multiply_fusion.1, f32[1024]{0:T(1024)S(1)} %copy-done.12, bf16[1024,4096]{1,0:T(8,128)(2,1)} %all-gather.5.cloned.1.call-done, f32[128,1024]{1,0:T(8,128)S(1)} %get-tuple-element.210, ...), kind=kOutput, calls=%fused_computation.107 | convolution fusion | flops 1080688512 | bytes 13374464 | tf_op jit(solution)/shard_map/tf,df->td/dot_general | solution.py:219
  299.7 1.0 fusion.54
  (67 shorter events, 8.9 us)
Async XLA Ops:
  7.2 58.6 %all-gather.5.cloned.1.call-start = ((), (), s32[]{:S(2)}) async-start(), calls=%async_computation.2 | async-start | bytes 9437184 | tf_op jit(solution)/shard_map/all_gather | solution.py:75
  7.9 93.0 %all-gather.7.cloned.1.call-start = ((), (), s32[]{:S(2)}) async-start(), calls=%async_computation.3 | async-start | bytes 1310720 | tf_op jit(solution)/shard_map/all_gather | solution.py:87
  72.8 2.9 copy-start.10
  72.8 57.7 %copy-start.9 = (f32[8,16]{1,0:T(8,128)S(1)}, f32[8,16]{1,0:T(8,128)}, u32[]{:S(2)}) copy-start(f32[8,16]{1,0:T(8,128)} %param.21) | copy-start | bytes 1540
  73.7 56.8 %all-gather.9.cloned.1.call-start = ((), (), s32[]{:S(2)}) async-start(), calls=%async_computation.4 | async-start | bytes 1310720 | tf_op jit(solution)/shard_map/all_gather | solution.py:88
  74.4 85.9 %all-gather.11.cloned.1.call-start = ((), (), s32[]{:S(2)}) async-start(), calls=%async_computation.5 | async-start | bytes 2359296 | tf_op jit(solution)/shard_map/all_gather | solution.py:76
  75.0 132.8 %reduce-scatter.5.cloned.1.call-start = ((), (), s32[]{:S(2)}) async-start(), calls=%async_computation.7 | async-start | bytes 2359296 | tf_op jit(solution)/shard_map/reduce_scatter | solution.py:138
  130.5 29.8 %copy-start.4 = (bf16[1,128,1024]{2,1,0:T(8,128)(2,1)S(1)}, bf16[1,128,1024]{2,1,0:T(8,128)(2,1)}, u32[]{:S(2)}) copy-start(bf16[1,128,1024]{2,1,0:T(8,128)(2,1)} %param.14) | copy-start | bytes 786436
  130.5 29.8 %copy-start.8 = (f32[1024]{0:T(1024)S(1)}, f32[1024]{0:T(1024)}, u32[]{:S(2)}) copy-start(f32[1024]{0:T(1024)} %param.20) | copy-start | bytes 12292
  130.6 4.6 %copy-start.2 = (bf16[512,1024]{1,0:T(8,128)(2,1)S(1)}, bf16[512,1024]{1,0:T(8,128)(2,1)}, u32[]{:S(2)}) copy-start(bf16[512,1024]{1,0:T(8,128)(2,1)} %get-tuple-element.159) | copy-start | bytes 3145732 | tf_op jit(solution)/shard_map/while/body/eval_jaxpr/cond
  167.1 76.8 %all-reduce.2.cloned.1.call-start = ((), (), s32[]{:S(2)}) async-start(), calls=%async_computation.8 | async-start | bytes 524288 | tf_op jit(solution)/shard_map/psum | solution.py:146
  207.8 83.4 %reduce-scatter.3.cloned.1.call-start = ((), (), s32[]{:S(2)}) async-start(), calls=%async_computation.6 | async-start | bytes 2621440 | tf_op jit(solution)/shard_map/reduce_scatter | solution.py:206
  208.2 1.3 copy-start.5
  212.0 4.3 %copy-start.7 = (bf16[128,1024]{0,1:T(8,128)(2,1)S(1)}, bf16[128,1024]{0,1:T(8,128)(2,1)}, u32[]{:S(2)}) copy-start(bf16[128,1024]{0,1:T(8,128)(2,1)} %copy.23) | copy-start | bytes 786436 | tf_op jit(solution)/shard_map/while/body/eval_jaxpr/cond
  216.3 1.2 copy-start.11
  219.1 1.6 copy-start.3
  221.3 4.0 %copy-start.1 = (bf16[1,128,1024]{2,1,0:T(8,128)(2,1)S(1)}, bf16[1,128,1024]{2,1,0:T(8,128)(2,1)}, u32[]{:S(2)}) copy-start(bf16[1,128,1024]{2,1,0:T(8,128)(2,1)} %param.13) | copy-start | bytes 786436
  225.3 1.6 copy-start
  228.1 64.4 %copy-start.6 = (f32[128,1024]{1,0:T(8,128)S(1)}, f32[128,1024]{1,0:T(8,128)}, u32[]{:S(2)}) copy-start(f32[128,1024]{1,0:T(8,128)} %get-tuple-element.205) | copy-start | bytes 1572868
  228.1 64.5 %copy-start.12 = (f32[1024]{0:T(1024)S(1)}, f32[1024]{0:T(1024)}, u32[]{:S(2)}) copy-start(f32[1024]{0:T(1024)} %param.19) | copy-start | bytes 12292
  291.2 1.7 copy-start.13
Sparse Core Ops, SparseCore 0:
  9.9 55.8 all-gather.4
  73.8 27.0 all-gather.6
  103.1 27.3 all-gather.8
  132.2 28.0 all-gather.10
  167.2 40.5 reduce-scatter.4
  210.0 33.8 all-reduce.1
  246.2 44.9 reduce-scatter.2
where the time goes:
time: 310 us; the launch traced here: 307 us
  waiting for transfers between devices  235 us (76%)
  matrix products  33.2 us (11%)
  between operations  14.9 us (5%)
  other arithmetic  13.1 us (4%)
  local copies, waits for them, and re-layouts  10.9 us (4%)
    all_gather x1, waiting for transfers between devices, per_device(): lax.all_gather(w_qkvu, 'dp', axis=0, tiled=True)  55.6 us
    reduce_scatter x1, waiting for transfers between devices, per_device(): lax.psum_scatter(key_terms.astype(jnp.bfloat16), 'seq', scatter_dimension...  45.5 us
    reduce_scatter x1, waiting for transfers between devices, per_device(): lax.psum_scatter(jnp.einsum('tr,tc->rc', mixed_rows, cot_rows, preferred_...  40.6 us
    all_gather x1, waiting for transfers between devices, per_device(): lax.all_gather(values_own, 'seq', axis=0, tiled=True)  29.5 us
    all_gather x1, waiting for transfers between devices, per_device(): lax.all_gather(keys_own, 'seq', axis=0, tiled=True)  25.1 us
    all_gather x1, waiting for transfers between devices, per_device(): lax.all_gather(w_out, 'dp', axis=0, tiled=True)  20.6 us
    psum x1, waiting for transfers between devices, per_device(): w_grad = lax.psum(grad_part, 'seq').astype(jnp.float32)  15.8 us
    dot_general x1, matrix products, per_device(): projected = jnp.dot(normed, w_full, preferred_element_type=jnp.float32)  7 us
  transfers between devices with their start and end apart: 7, of which 7 were waited for; matrix products, arithmetic and copies ran while one was open for 10% of the time, Pallas kernels for 0%

commit v1 on v0

--- a/solution.py
+++ b/solution.py
@@ -1,6 +1,8 @@
 import jax
 import jax.numpy as jnp
 from jax import lax
+from jax.experimental import pallas as pl
+from jax.experimental.pallas import tpu as pltpu
 from jax.sharding import PartitionSpec as P
 
 H = 8
@@ -222,9 +224,560 @@
     return (mixed[None], input_grad[None], w_grad)
 
 
+MESH = pl.DeviceIdType.MESH
+VM = pl.BlockSpec(memory_space=pltpu.VMEM)
+F32 = jnp.float32
+BF16 = jnp.bfloat16
+
+
+def plane_of(stream):
+    chip, core = stream // 2, stream % 2
+    mid = 1 - ((chip + 1) // 2) % 2
+    return mid * (1 + core) + (1 - mid) * 3 * core
+
+
+def plane_sources(plane):
+    mid = ((plane + 1) // 2) % 2
+    core = mid * (plane - 1) + (1 - mid) * (plane // 3)
+    return core, (1 - mid, 2 + mid)
+
+
+def remote(src, dst, send_sem, recv_sem, target):
+    return pltpu.make_async_remote_copy(
+        src_ref=src,
+        dst_ref=dst,
+        send_sem=send_sem,
+        recv_sem=recv_sem,
+        device_id=target,
+        device_id_type=MESH,
+    )
+
+
+def gather_kernel(
+    n_dp, n_seq, x_ref, c_ref, w_ref, m_ref, xo_ref, co_ref, wo_ref, mo_ref,
+    zsend, fsend, frecv, wsend, wrecv, msend, mrecv, local_sem,
+):
+    me = lax.axis_index("dp")
+    z = lax.axis_index("seq")
+    chip, core = me // 2, me % 2
+    cy, cx = chip // 2, chip % 2
+    x_chip, y_chip = 2 * cy + (1 - cx), 2 * (1 - cy) + cx
+    sibling = 2 * chip + (1 - core)
+    rows = w_ref.shape[0]
+    width = x_ref.shape[1]
+    home = plane_of(me)
+    slot = chip // 2
+    src_core, chips = plane_sources(z)
+    ins, outs = (x_ref, c_ref), (xo_ref, co_ref)
+
+    def z_send(a, s):
+        return remote(ins[a], outs[a].at[slot, s], zsend.at[a], frecv.at[a, slot, s], (me, home))
+
+    def own_copy(a):
+        return pltpu.make_async_copy(ins[a], outs[a].at[slot, z], local_sem.at[a])
+
+    def w_send(peer, group):
+        return remote(
+            w_ref.at[:, pl.ds(pl.multiple_of(group * width + peer * DH, DH), DH)],
+            wo_ref.at[pl.ds(pl.multiple_of(me * rows, rows), rows), pl.ds(group * DH, DH)],
+            wsend.at[peer, group],
+            wrecv.at[me, group],
+            (peer, z),
+        )
+
+    def w_arrive(peer, group):
+        return remote(
+            w_ref.at[:, pl.ds(pl.multiple_of(group * width + me * DH, DH), DH)],
+            wo_ref.at[pl.ds(pl.multiple_of(peer * rows, rows), rows), pl.ds(group * DH, DH)],
+            wsend.at[peer, group],
+            wrecv.at[peer, group],
+            (peer, z),
+        )
+
+    def w_own(group):
+        return pltpu.make_async_copy(
+            w_ref.at[:, pl.ds(pl.multiple_of(group * width + me * DH, DH), DH)],
+            wo_ref.at[pl.ds(pl.multiple_of(me * rows, rows), rows), pl.ds(group * DH, DH)],
+            local_sem.at[3 + group],
+        )
+
+    def m_send(peer):
+        return remote(m_ref, mo_ref.at[slot], msend.at[peer], mrecv.at[slot], (peer, z))
+
+    def m_own():
+        return pltpu.make_async_copy(m_ref, mo_ref.at[slot], local_sem.at[2])
+
+    @pl.when(home != z)
+    def _():
+        z_send(0, z).start()
+
+    @pl.when(home == z)
+    def _():
+        own_copy(0).start()
+        m_own().start()
+
+    for step in range(1, n_dp):
+        peer = lax.rem(me + step, n_dp)
+
+        @pl.when(home == z)
+        def _():
+            m_send(peer).start()
+
+        for group in range(4):
+            w_send(peer, group).start()
+    for group in range(4):
+        w_own(group).start()
+
+    @pl.when(home != z)
+    def _():
+        z_send(1, z).start()
+
+    @pl.when(home == z)
+    def _():
+        own_copy(1).start()
+
+    def forwards(a, j, b):
+        block = outs[a].at[j, b]
+        owner = chips[j]
+        mine = core == src_core
+
+        def to(target, leg):
+            return remote(block, block, fsend.at[a, j, b, leg], frecv.at[a, j, b], (target, z))
+
+        via_y = (chip == owner) | ((x_chip == owner) & (b < n_seq // 2))
+        via_x = (chip == owner) | ((y_chip == owner) & (b >= n_seq // 2))
+        return (
+            (mine & via_x, to(2 * x_chip + core, 0)),
+            (mine & via_y, to(2 * y_chip + core, 1)),
+            (mine, to(sibling, 2)),
+        )
+
+    for a in range(2):
+        for b in range(n_seq):
+            for j in range(2):
+                block = outs[a].at[j, b]
+                held = (me == 2 * chips[j] + src_core) & (z == b)
+
+                @pl.when(held)
+                def _():
+                    own_copy(a).wait()
+
+                @pl.when(jnp.logical_not(held))
+                def _():
+                    remote(block, block, zsend.at[a], frecv.at[a, j, b], (me, z)).wait_recv()
+
+                for use, copy in forwards(a, j, b):
+
+                    @pl.when(use)
+                    def _():
+                        copy.start()
+
+    for step in range(1, n_dp):
+        peer = lax.rem(me + step, n_dp)
+        for group in range(4):
+            w_arrive(peer, group).wait_recv()
+            w_send(peer, group).wait_send()
+
+        @pl.when(home == z)
+        def _():
+            m_send(peer).wait_send()
+
+    for group in range(4):
+        w_own(group).wait()
+
+    @pl.when(home == z)
+    def _():
+        m_own().wait()
+
+    for j in range(2):
+
+        @pl.when(jnp.logical_not((home == z) & (slot == j)))
+        def _():
+            remote(m_ref, mo_ref.at[j], msend.at[0], mrecv.at[j], (me, z)).wait_recv()
+
+    for a in range(2):
+
+        @pl.when(home != z)
+        def _():
+            z_send(a, z).wait_send()
+
+        for b in range(n_seq):
+            for j in range(2):
+                for use, copy in forwards(a, j, b):
+
+                    @pl.when(use)
+                    def _():
+                        copy.wait_send()
+
+
+def stats_kernel(n_dp, s_ref, o_ref, send, recv, local_sem):
+    me = lax.axis_index("dp")
+    z = lax.axis_index("seq")
+    own = pltpu.make_async_copy(s_ref, o_ref.at[me], local_sem)
+    own.start()
+    for step in range(1, n_dp):
+        peer = lax.rem(me + step, n_dp)
+        remote(s_ref, o_ref.at[me], send.at[peer], recv.at[me], (peer, z)).start()
+    own.wait()
+    for step in range(1, n_dp):
+        peer = lax.rem(me + step, n_dp)
+        copy = remote(s_ref, o_ref.at[peer], send.at[peer], recv.at[peer], (peer, z))
+        copy.wait_recv()
+        copy.wait_send()
+
+
+def reduce_kernel(
+    n_dp, n_seq, p_ref, g_ref, o_ref, go_ref, pair, mixed_up, landed, final, g_land, g_sum,
+    psend, precv, csend, crecv, osend, orecv, gsend, grecv, hsend, hrecv, local_sem,
+):
+    me = lax.axis_index("dp")
+    z = lax.axis_index("seq")
+    chip, core = me // 2, me % 2
+    sibling = 2 * chip + (1 - core)
+    chips_n = n_dp // 2
+    g_rows = g_ref.shape[0] // n_seq
+
+    def g_slice(ref, index):
+        return ref.at[pl.ds(pl.multiple_of(index * g_rows, g_rows), g_rows)]
+
+    def pair_send(part, c):
+        return remote(
+            p_ref.at[part, 2 * c + (1 - core)], pair.at[part, c],
+            psend.at[part, c], precv.at[part, c], (sibling, z),
+        )
+
+    def cross_send(part, c):
+        return remote(
+            mixed_up.at[part, c], landed.at[part, chip],
+            csend.at[part, c], crecv.at[part, chip], (2 * c + core, z),
+        )
+
+    def cross_arrive(part, c):
+        return remote(
+            mixed_up.at[part, c], landed.at[part, c],
+            csend.at[part, c], crecv.at[part, c], (2 * c + core, z),
+        )
+
+    def g_send(peer):
+        return remote(
+            g_slice(g_ref, peer), g_land.at[z], gsend.at[peer], grecv.at[z], (me, peer)
+        )
+
+    def g_arrive(peer):
+        return remote(
+            g_slice(g_ref, peer), g_land.at[peer], gsend.at[peer], grecv.at[peer], (me, peer)
+        )
+
+    def h_send(peer):
+        return remote(g_sum, g_slice(go_ref, z), hsend.at[peer], hrecv.at[z], (me, peer))
+
+    def h_arrive(peer):
+        return remote(g_sum, g_slice(go_ref, peer), hsend.at[peer], hrecv.at[peer], (me, peer))
+
+    others = [lax.rem(chip + step, chips_n) for step in range(1, chips_n)]
+    peers = [lax.rem(z + step, n_seq) for step in range(1, n_seq)]
+    parts = p_ref.shape[0]
+    for part in range(parts):
+        for c in others + [chip]:
+            pair_send(part, c).start()
+    for peer in peers:
+        g_send(peer).start()
+    for part in range(parts):
+        for c in others + [chip]:
+            pair_send(part, c).wait_recv()
+            mixed_up[part, c] = (
+                p_ref[part, 2 * c + core].astype(F32) + pair[part, c].astype(F32)
+            ).astype(BF16)
+            if c is not chip:
+                cross_send(part, c).start()
+    total = g_slice(g_ref, z)[...].astype(F32)
+    for peer in peers:
+        g_arrive(peer).wait_recv()
+        total = total + g_land[peer].astype(F32)
+    g_sum[...] = total.astype(BF16)
+    own_g = pltpu.make_async_copy(g_sum, g_slice(go_ref, z), local_sem.at[0])
+    own_g.start()
+    for peer in peers:
+        h_send(peer).start()
+    block, half = me % n_seq, me // n_seq
+    src_core, sources = plane_sources(z)
+    stream = 2 * ((1 - half) * sources[0] + half * sources[1]) + src_core
+    stays = (stream == me) & (block == z)
+    gone = jnp.logical_not(stays)
+    home = plane_of(me)
+    from_dp = (chip // 2) * n_seq + z
+    arrives = jnp.logical_not((home == z) & (from_dp == me))
+
+    def final_send(part):
+        return remote(
+            final.at[part], o_ref.at[part], osend.at[part], orecv.at[part], (stream, block)
+        )
+
+    def final_own(part):
+        return pltpu.make_async_copy(final.at[part], o_ref.at[part], local_sem.at[1 + part])
+
+    for part in range(parts):
+        total = mixed_up[part, chip].astype(F32)
+        for c in others:
+            cross_arrive(part, c).wait_recv()
+            total = total + landed[part, c].astype(F32)
+        final[part] = total.astype(BF16)
+
+        @pl.when(gone)
+        def _():
+            final_send(part).start()
+
+        @pl.when(stays)
+        def _():
+            final_own(part).start()
+
+    for part in range(parts):
+        for c in others + [chip]:
+            pair_send(part, c).wait_send()
+        for c in others:
+            cross_send(part, c).wait_send()
+
+        @pl.when(gone)
+        def _():
+            final_send(part).wait_send()
+
+        @pl.when(stays)
+        def _():
+            final_own(part).wait()
+
+        @pl.when(arrives)
+        def _():
+            final_send(part).wait_recv()
+
+    own_g.wait()
+    for peer in peers:
+        g_send(peer).wait_send()
+        h_send(peer).wait_send()
+        h_arrive(peer).wait_recv()
+
+
+def mm(a, b, dims):
+    return lax.dot_general(a, b, (dims, ((), ())), preferred_element_type=F32)
+
+
+def forward_kernel(
+    bias_ref, len_ref, proj_ref, srow_ref, scol_ref, att_ref, weight_ref, slope_ref
+):
+    length = len_ref[pl.program_id(0)]
+    head = lax.axis_index("dp")
+    total = proj_ref.shape[1]
+    rows = total // 4
+    acts = [jax.nn.silu(proj_ref[0, :, (1 + g) * DH : (2 + g) * DH]).astype(BF16) for g in range(3)]
+    values, queries, keys = acts
+    for start in range(0, total, rows):
+        end = start + rows
+        scores = mm(queries[start:end], keys[:end], ((1,), (1,))) * DH ** (-0.5)
+        elapsed = scol_ref[0, start:end, :] - srow_ref[0, :, :end]
+        bias = jnp.full(elapsed.shape, bias_ref[head, 0], F32)
+        for degree in range(1, bias_ref.shape[1]):
+            bias = jnp.where(elapsed >= 2**degree - 1, bias_ref[head, degree], bias)
+        scores = scores + bias
+        pos_q = start + lax.broadcasted_iota(jnp.int32, elapsed.shape, 0)
+        pos_k = lax.broadcasted_iota(jnp.int32, elapsed.shape, 1)
+        allowed = (pos_k <= pos_q) & (pos_k < length) & (pos_q < length)
+        sig = jax.nn.sigmoid(scores)
+        weight = jnp.where(allowed, scores * sig, 0.0).astype(BF16)
+        weight_ref[0, start:end, :end] = weight
+        slope_ref[0, start:end, :end] = jnp.where(allowed, sig * (1.0 + scores * (1.0 - sig)), 0.0)
+        att_ref[0, start:end, :] = mm(weight, values[:end], ((1,), (0,)))
+
+
+def backward_kernel(proj_ref, datt_ref, dgate_ref, weight_ref, slope_ref, out_ref, k_acc, v_acc):
+    total = proj_ref.shape[1]
+    rows = total // 4
+    acts = [jax.nn.silu(proj_ref[0, :, (1 + g) * DH : (2 + g) * DH]).astype(BF16) for g in range(3)]
+    values, queries, keys = acts
+    scale = DH ** (-0.5)
+
+    def put(group, start, end, grad):
+        cols = slice(group * DH, (group + 1) * DH)
+        out_ref[0, start:end, cols] = (grad * silu_slope(proj_ref[0, start:end, cols])).astype(BF16)
+
+    for start in reversed(range(0, total, rows)):
+        end = start + rows
+        d_att = datt_ref[0, start:end, :]
+        d_weight = mm(d_att, values[:end], ((1,), (1,)))
+        d_scores = (d_weight * slope_ref[0, start:end, :end]).astype(BF16)
+        put(2, start, end, mm(d_scores, keys[:end], ((1,), (0,))) * scale)
+        k_part = mm(d_scores, queries[start:end], ((0,), (0,)))
+        v_part = mm(weight_ref[0, start:end, :end], d_att, ((0,), (0,)))
+        if end == total:
+            k_acc[...] = k_part
+            v_acc[...] = v_part
+        else:
+            k_acc[:end] += k_part
+            v_acc[:end] += v_part
+    put(0, 0, total, dgate_ref[0])
+    put(1, 0, total, v_acc[...])
+    put(3, 0, total, k_acc[...] * scale)
+
+
+def head_parallel(
+    n_dp, n_seq, tokens, cotangent, stamps, lengths, w_qkvu, w_out, gain_in, gain_out, bias_table
+):
+    tok, width = tokens.shape[1:]
+    seq_len = stamps.shape[1]
+    head = lax.axis_index("dp")
+    meta = jnp.concatenate([stamps.reshape(-1, DH), jnp.broadcast_to(lengths[:, None], (4, DH))])
+    dma = pltpu.SemaphoreType.DMA
+    sds = jax.ShapeDtypeStruct
+    side = pltpu.CompilerParams(has_side_effects=True)
+    x_all, c_all, w_head, metas = pl.pallas_call(
+        lambda *refs: gather_kernel(n_dp, n_seq, *refs),
+        out_shape=(
+            sds((2, n_seq, tok, width), BF16),
+            sds((2, n_seq, tok, width), BF16),
+            sds((width, 4 * DH), BF16),
+            sds((2,) + meta.shape, jnp.int32),
+        ),
+        in_specs=[VM] * 4,
+        out_specs=[VM] * 4,
+        scratch_shapes=[
+            dma((2,)),
+            dma((2, 2, n_seq, 3)),
+            dma((2, 2, n_seq)),
+            dma((n_dp, 4)),
+            dma((n_dp, 4)),
+            dma((n_dp,)),
+            dma((2,)),
+            dma((7,)),
+        ],
+        compiler_params=side,
+        name="gather",
+    )(tokens[0], cotangent[0], w_qkvu, meta)
+    count = 2 * seq_len
+    x_rows = x_all.reshape(count, width)
+    c_rows = c_all.reshape(count, width)
+    stamp_rows = metas[:, : seq_len // DH].reshape(2, 1, seq_len)
+    stamp_cols = stamp_rows.reshape(2, seq_len, 1)
+    spans = metas[:, seq_len // DH, 0]
+    normed = layer_norm(x_rows.astype(F32), gain_in).astype(BF16)
+    projected = jnp.dot(normed, w_head, preferred_element_type=F32)
+    proj3 = projected.reshape(2, seq_len, 4 * DH)
+    smem = pl.BlockSpec(memory_space=pltpu.SMEM)
+
+    def per(*shape):
+        return pl.BlockSpec((1,) + shape, lambda i: (i,) + (0,) * len(shape))
+
+    attended, weight, slope = pl.pallas_call(
+        forward_kernel,
+        grid=(2,),
+        out_shape=(
+            sds((2, seq_len, DH), F32),
+            sds((2, seq_len, seq_len), BF16),
+            sds((2, seq_len, seq_len), F32),
+        ),
+        in_specs=[smem, smem, per(seq_len, 4 * DH), per(1, seq_len), per(seq_len, 1)],
+        out_specs=[per(seq_len, DH), per(seq_len, seq_len), per(seq_len, seq_len)],
+        name="forward",
+    )(bias_table, spans, proj3, stamp_rows, stamp_cols)
+    att = attended.reshape(count, DH)
+    gate = jax.nn.silu(projected[:, :DH])
+    gain_head = lax.dynamic_slice_in_dim(gain_out, head * DH, DH)
+    d_mix = lax.dot_general(c_rows, w_out, (((1,), (1,)), ((), ())), preferred_element_type=F32)
+    g = d_mix * gate * gain_head
+    mean_own = jnp.mean(att, axis=1)
+    off = att - mean_own[:, None]
+    stats = jnp.stack(
+        [mean_own, jnp.sum(off * off, axis=1), jnp.sum(g, axis=1), jnp.sum(g * off, axis=1)]
+    )
+    gathered = pl.pallas_call(
+        lambda *refs: stats_kernel(n_dp, *refs),
+        out_shape=sds((n_dp, 4, count // DH, DH), F32),
+        in_specs=[VM],
+        out_specs=VM,
+        scratch_shapes=[dma((n_dp,)), dma((n_dp,)), dma],
+        compiler_params=side,
+        name="stats",
+    )(stats.reshape(4, count // DH, DH))
+    means, squares, g_sums, g_offs = [gathered[:, k] for k in range(4)]
+    mean = jnp.mean(means, axis=0)
+    shift = means - mean[None]
+    variance = jnp.sum(squares + DH * shift * shift, axis=0) / width
+    rstd = lax.rsqrt(variance + EPS)
+    g_mean = jnp.sum(g_sums, axis=0) / width
+    g_dot = rstd * jnp.sum(g_offs + shift * g_sums, axis=0) / width
+    mean, rstd, g_mean, g_dot = [v.reshape(count, 1) for v in (mean, rstd, g_mean, g_dot)]
+    hat = (att - mean) * rstd
+    normed_att = hat * gain_head
+    mixed_rows = (normed_att * gate).astype(BF16)
+    d_gate = d_mix * normed_att
+    d_att = (rstd * (g - g_mean - hat * g_dot)).astype(BF16)
+    d_proj = pl.pallas_call(
+        backward_kernel,
+        grid=(2,),
+        out_shape=sds((2, seq_len, 4 * DH), BF16),
+        in_specs=[
+            per(seq_len, 4 * DH),
+            per(seq_len, DH),
+            per(seq_len, DH),
+            per(seq_len, seq_len),
+            per(seq_len, seq_len),
+        ],
+        out_specs=per(seq_len, 4 * DH),
+        scratch_shapes=[pltpu.VMEM((seq_len, DH), F32)] * 2,
+        name="backward",
+    )(proj3, d_att.reshape(2, seq_len, DH), d_gate.reshape(2, seq_len, DH), weight, slope)
+    mixed_part = jnp.dot(mixed_rows, w_out, preferred_element_type=F32).astype(BF16)
+    d_part = lax.dot_general(
+        d_proj.reshape(count, 4 * DH), w_head, (((1,), (1,)), ((), ())), preferred_element_type=F32
+    ).astype(BF16)
+    w_part = lax.dot_general(
+        mixed_rows, c_rows, (((0,), (0,)), ((), ())), preferred_element_type=F32
+    ).astype(BF16)
+    shape = (n_dp, tok, width)
+    half = n_dp // 2
+    sums, w_sum = pl.pallas_call(
+        lambda *refs: reduce_kernel(n_dp, n_seq, *refs),
+        out_shape=(sds((2, tok, width), BF16), sds(w_part.shape, BF16)),
+        in_specs=[VM] * 2,
+        out_specs=[VM] * 2,
+        scratch_shapes=[
+            pltpu.VMEM((2, half, tok, width), BF16),
+            pltpu.VMEM((2, half, tok, width), BF16),
+            pltpu.VMEM((2, half, tok, width), BF16),
+            pltpu.VMEM((2, tok, width), BF16),
+            pltpu.VMEM((n_seq, w_part.shape[0] // n_seq, width), BF16),
+            pltpu.VMEM((w_part.shape[0] // n_seq, width), BF16),
+            dma((2, half)),
+            dma((2, half)),
+            dma((2, half)),
+            dma((2, half)),
+            dma((2,)),
+            dma((2,)),
+            dma((n_seq,)),
+            dma((n_seq,)),
+            dma((n_seq,)),
+            dma((n_seq,)),
+            dma((3,)),
+        ],
+        compiler_params=side,
+        name="reduce",
+    )(jnp.stack([mixed_part.reshape(shape), d_part.reshape(shape)]), w_part)
+    wide_rows = tokens[0].astype(F32)
+    mixed = (wide_rows + sums[0].astype(F32)).astype(BF16)
+    unused_rows, in_back = jax.vjp(lambda values: layer_norm(values, gain_in), wide_rows)
+    back = in_back(sums[1].astype(F32))[0]
+    input_grad = (cotangent[0].astype(F32) + back).astype(BF16)
+    return (mixed[None], input_grad[None], w_sum.astype(F32))
+
+
 def solution(mesh):
+    n_dp, n_seq = mesh.shape["dp"], mesh.shape["seq"]
+
+    def body(*args):
+        streams_fit = n_dp == 2 * n_seq and n_dp == H and args[5].shape[0] == DH
+        if streams_fit and args[2].shape[0] == 1:
+            return head_parallel(n_dp, n_seq, *args)
+        return per_device(*args)
+
     return jax.shard_map(
-        per_device,
+        body,
         mesh=mesh,
         in_specs=(
             P("dp", "seq", None),

time: 310 us -> 303 us (0.977)
  Pallas kernels: 0 us -> 268 us
  waiting for transfers between devices: 235 us -> 0 us
  matrix products: 33.2 us -> 10.4 us
  between operations: 14.9 us -> 1.53 us
  local copies, waits for them, and re-layouts: 10.9 us -> 4.54 us
  other arithmetic: 13.1 us -> 17.8 us
    pallas_call x0 -> x5, Pallas kernels: none -> 268 us  [the longest x1 195 us: head_parallel(): pl.pallas_call(lambda *refs: gather_kernel(n_dp, n_seq, *refs), out_shape...]
    all_gather x4 -> x0, waiting for transfers between devices: 131 us -> none  [the longest x1 55.6 us: per_device(): lax.all_gather(w_qkvu, 'dp', axis=0, tiled=True)]
    reduce_scatter x2 -> x0, waiting for transfers between devices: 86.1 us -> none  [the longest x1 45.5 us: per_device(): lax.psum_scatter(key_terms.astype(jnp.bfloat16), 'seq', scatter_dimension...]
    dot_general x13 -> x5, matrix products: 33.2 us -> 10.4 us  [the longest x1 3.41 us: head_parallel(): lax.dot_general(c_rows, w_out, (((1,), (1,)), ((), ())), preferred_elemen...]
    psum x1 -> x0, waiting for transfers between devices: 15.8 us -> none  [per_device(): w_grad = lax.psum(grad_part, 'seq').astype(jnp.float32)]
    cond x11 -> x0, local copies, waits for them, and re-layouts: 4.58 us -> none  [the longest x1 4 us: guarded(): return lax.cond(active, action, lambda same: same, state)]
    convert_element_type x2 -> x4, other arithmetic: 1.89 us -> 6.2 us  [the longest x1 2.64 us: head_parallel(): mixed_rows = (normed_att * gate).astype(BF16)]
    reduce_sum x0 -> x4, other arithmetic: none -> 3.26 us  [the longest x1 1.25 us: head_parallel(): mean_own = jnp.mean(att, axis=1)]
  transfers between devices with their start and end apart: 7 -> 0, of which waited for: 7 -> 0; matrix products, arithmetic and copies ran while one was open for 10% -> 0% of each run, Pallas kernels for 0% -> 0%
where the time goes in v1:
time: 303 us; the launch traced here: 302 us
  Pallas kernels  268 us (88%)
  other arithmetic  17.8 us (6%)
  matrix products  10.4 us (3%)
  local copies, waits for them, and re-layouts  4.54 us (1%)
    pallas_call x1, Pallas kernels, head_parallel(): pl.pallas_call(lambda *refs: gather_kernel(n_dp, n_seq, *refs), out_shape...  195 us
    pallas_call x1, Pallas kernels, head_parallel(): pl.pallas_call(lambda *refs: reduce_kernel(n_dp, n_seq, *refs), out_shape...  55.6 us
    pallas_call x1, Pallas kernels, head_parallel(): pl.pallas_call(lambda *refs: stats_kernel(n_dp, *refs), out_shape=sds((n_...  6.95 us

profile of v1, /device:TPU:3, one launch (start us, length us, event | category | flops | bytes accessed | tf_op | source)
XLA Modules:
  0.0 302.4 jit_solution(16297225402971368602)
XLA Ops:
  0.6 0.0 copy-start
  1.3 1.3 concatenate.4.refs_3_
  2.6 195.3 %gather.1 = (bf16[2,4,128,1024]{3,2,1,0:T(8,128)(2,1)}, bf16[2,4,128,1024]{3,2,1,0:T(8,128)(2,1)}, bf16[1024,512]{1,0:T(8,128)(2,1)}, s32[2,8,128]{2,1,0:T(8,128)}) custom-call(bf16[128,1024]{1,0:T(8,128)(2,1)} %bitcast.110, bf16[128,1024]{1,0:T(8,128)(2,1)} %bitcast.117, bf16[128,4096]{1,0:T(8,128)(2,1)} %refs_2_.1, s32[8,128]{1,0:T(8,128)} %concatenate.4.refs_3_), custom_call_target="tpu_custom_call" | custom-call | tf_op jit(solution)/shard_map/gather/pallas_call | solution.py:630
  198.0 2.1 convert_reduce_fusion
  200.0 0.1 copy-done.1
  200.2 0.7 multiply_reduce_fusion
  200.9 0.7 fusion.2
  201.6 0.5 copy-done.11
  202.1 2.6 fusion.29
  204.7 1.1 reshape_reshape.4.scol_ref
  205.9 0.6 slice_reduce_fusion.len_ref
  206.5 5.0 %forward.1 = (f32[2,512,128]{2,1,0:T(8,128)}, bf16[2,512,512]{2,1,0:T(8,128)(2,1)}, f32[2,512,512]{2,1,0:T(8,128)}) custom-call(f32[8,16]{1,0:T(8,128)} %bias_ref.1, s32[2]{0:T(128)} %slice_reduce_fusion.len_ref, f32[2,512,512]{2,1,0:T(8,128)} %bitcast.107, s32[2,1,512]{2,1,0:T(1,128)} %bitcast.118, s32[2,512,1]{2,1,0:T(8,128)} %reshape_reshape.4.scol_ref), custom_call_target="tpu_custom_call" | custom-call | tf_op jit(solution)/shard_map/forward/pallas_call | solution.py:667
  211.5 1.3 reduce_sum.138
  212.8 0.8 dynamic_slice.3
  213.6 3.4 %fusion.28 = (f32[1024]{0:T(1024)S(1)}, f32[1024]{0:T(1024)S(1)}, f32[1024,128]{1,0:T(8,128)}, f32[1024,128]{1,0:T(8,128)}) fusion(f32[1024]{0:T(1024)S(1)} %bitcast.121, f32[2,512,128]{2,1,0:T(8,128)} %get-tuple-element.15, f32[128]{0:T(128)S(1)} %dynamic_slice.3, f32[1024,512]{1,0:T(8,128)S(1)} %copy-done.2, bf16[1024,1024]{1,0:T(8,128)(2,1)} %bitcast.111, ...), kind=kOutput, calls=%fused_computation.69 | convolution fusion | flops 269744128 | bytes 4469248 | tf_op jit(solution)/shard_map/dot_general | solution.py:682
  217.0 0.4 multiply_reduce_fusion.1
  217.4 0.6 pad_maximum_fusion.1.refs_0_
  218.0 6.9 %stats.1 = f32[8,4,8,128]{3,2,1,0:T(8,128)} custom-call(f32[4,8,128]{2,1,0:T(8,128)} %pad_maximum_fusion.1.refs_0_), custom_call_target="tpu_custom_call" | custom-call | tf_op jit(solution)/shard_map/stats/pallas_call | solution.py:689
  224.9 0.8 bitcast_reduce_fusion
  225.8 0.8 fusion.21
  226.6 2.6 multiply_convert_fusion.1
  229.3 5.2 %backward.1 = bf16[2,512,512]{2,1,0:T(8,128)(2,1)} custom-call(f32[2,512,512]{2,1,0:T(8,128)} %bitcast.108, bf16[2,512,128]{2,1,0:T(8,128)(2,1)} %bitcast.115, f32[2,512,128]{2,1,0:T(8,128)} %bitcast.113, bf16[2,512,512]{2,1,0:T(8,128)(2,1)} %get-tuple-element.17.weight_ref, f32[2,512,512]{2,1,0:T(8,128)} %get-tuple-element.18.slope_ref), custom_call_target="tpu_custom_call" | custom-call | tf_op jit(solution)/shard_map/backward/pallas_call | solution.py:711
  234.5 2.5 convolution_convert_fusion
  237.0 0.7 convolution_convert_fusion.1
  237.7 2.3 pad_maximum_fusion.refs_0_
  240.0 1.2 convolution_convert_fusion.2.refs_1_
  241.2 55.6 %reduce.9 = (bf16[2,128,1024]{2,1,0:T(8,128)(2,1)}, bf16[128,1024]{1,0:T(8,128)(2,1)}) custom-call(bf16[2,8,128,1024]{3,2,1,0:T(8,128)(2,1)} %pad_maximum_fusion.refs_0_, bf16[128,1024]{1,0:T(8,128)(2,1)} %convolution_convert_fusion.2.refs_1_), custom_call_target="tpu_custom_call" | custom-call | tf_op jit(solution)/shard_map/reduce/pallas_call | solution.py:735
  296.9 0.1 convert_reduce_fusion.1
  297.0 1.2 fusion.11
  298.2 1.2 fusion.16
  299.5 2.0 fusion.15
  301.5 0.8 convert_element_type.81
  (36 shorter events, 0.1 us)
Async XLA Ops:
  0.6 212.9 %copy-start = (bf16[128,1024]{1,0:T(8,128)(2,1)S(1)}, bf16[128,1024]{1,0:T(8,128)(2,1)}, u32[]{:S(2)}) copy-start(bf16[128,1024]{1,0:T(8,128)(2,1)} %param.14) | copy-start | bytes 786436
  197.9 2.2 copy-start.1
  197.9 2.9 copy-start.8
  200.9 1.2 copy-start.11
  202.1 2.6 copy-start.10
  204.7 8.9 %copy-start.2 = (f32[1024,512]{1,0:T(8,128)S(1)}, f32[1024,512]{1,0:T(8,128)}, u32[]{:S(2)}) copy-start(f32[1024,512]{1,0:T(8,128)} %fusion.29) | copy-start | bytes 6291460
  204.7 1.8 copy-start.9
  213.6 3.4 %copy-start.4 = (f32[2,512,128]{2,1,0:T(8,128)S(1)}, f32[2,512,128]{2,1,0:T(8,128)}, u32[]{:S(2)}) copy-start(f32[2,512,128]{2,1,0:T(8,128)} %get-tuple-element.15) | copy-start | bytes 1572868
  229.3 5.2 %copy-start.12 = (bf16[1024,512]{1,0:T(8,128)(2,1)S(1)}, bf16[1024,512]{1,0:T(8,128)(2,1)}, u32[]{:S(2)}) copy-start(bf16[1024,512]{1,0:T(8,128)(2,1)} %get-tuple-element.14) | copy-start | bytes 3145732
  237.7 2.3 copy-start.5
  241.2 55.7 %copy-start.3 = (bf16[1,128,1024]{2,1,0:T(8,128)(2,1)S(1)}, bf16[1,128,1024]{2,1,0:T(8,128)(2,1)}, u32[]{:S(2)}) copy-start(bf16[1,128,1024]{2,1,0:T(8,128)(2,1)} %param.9) | copy-start | bytes 786436
  241.2 58.2 %copy-start.6 = (bf16[1,128,1024]{2,1,0:T(8,128)(2,1)S(1)}, bf16[1,128,1024]{2,1,0:T(8,128)(2,1)}, u32[]{:S(2)}) copy-start(bf16[1,128,1024]{2,1,0:T(8,128)(2,1)} %param.10) | copy-start | bytes 786436
  296.9 4.7 %copy-start.7 = (bf16[128,1024]{1,0:T(8,128)(2,1)S(1)}, bf16[128,1024]{1,0:T(8,128)(2,1)}, u32[]{:S(2)}) copy-start(bf16[128,1024]{1,0:T(8,128)(2,1)} %get-tuple-element.20) | copy-start | bytes 786436

commit v2 on v1

--- a/solution.py
+++ b/solution.py
@@ -263,8 +263,6 @@
     cy, cx = chip // 2, chip % 2
     x_chip, y_chip = 2 * cy + (1 - cx), 2 * (1 - cy) + cx
     sibling = 2 * chip + (1 - core)
-    rows = w_ref.shape[0]
-    width = x_ref.shape[1]
     home = plane_of(me)
     slot = chip // 2
     src_core, chips = plane_sources(z)
@@ -276,30 +274,14 @@
     def own_copy(a):
         return pltpu.make_async_copy(ins[a], outs[a].at[slot, z], local_sem.at[a])
 
-    def w_send(peer, group):
-        return remote(
-            w_ref.at[:, pl.ds(pl.multiple_of(group * width + peer * DH, DH), DH)],
-            wo_ref.at[pl.ds(pl.multiple_of(me * rows, rows), rows), pl.ds(group * DH, DH)],
-            wsend.at[peer, group],
-            wrecv.at[me, group],
-            (peer, z),
-        )
-
-    def w_arrive(peer, group):
-        return remote(
-            w_ref.at[:, pl.ds(pl.multiple_of(group * width + me * DH, DH), DH)],
-            wo_ref.at[pl.ds(pl.multiple_of(peer * rows, rows), rows), pl.ds(group * DH, DH)],
-            wsend.at[peer, group],
-            wrecv.at[peer, group],
-            (peer, z),
-        )
-
-    def w_own(group):
-        return pltpu.make_async_copy(
-            w_ref.at[:, pl.ds(pl.multiple_of(group * width + me * DH, DH), DH)],
-            wo_ref.at[pl.ds(pl.multiple_of(me * rows, rows), rows), pl.ds(group * DH, DH)],
-            local_sem.at[3 + group],
-        )
+    def w_send(peer):
+        return remote(w_ref.at[peer], wo_ref.at[me], wsend.at[peer], wrecv.at[me], (peer, z))
+
+    def w_arrive(peer):
+        return remote(w_ref.at[peer], wo_ref.at[peer], wsend.at[peer], wrecv.at[peer], (peer, z))
+
+    def w_own():
+        return pltpu.make_async_copy(w_ref.at[me], wo_ref.at[me], local_sem.at[3])
 
     def m_send(peer):
         return remote(m_ref, mo_ref.at[slot], msend.at[peer], mrecv.at[slot], (peer, z))
@@ -323,10 +305,8 @@
         def _():
             m_send(peer).start()
 
-        for group in range(4):
-            w_send(peer, group).start()
-    for group in range(4):
-        w_own(group).start()
+        w_send(peer).start()
+    w_own().start()
 
     @pl.when(home != z)
     def _():
@@ -336,37 +316,54 @@
     def _():
         own_copy(1).start()
 
-    def forwards(a, j, b):
+    def order(i):
+        return lax.rem(z + i, n_seq)
+
+    def pass_on(a, j, b, target, leg):
         block = outs[a].at[j, b]
-        owner = chips[j]
-        mine = core == src_core
-
-        def to(target, leg):
-            return remote(block, block, fsend.at[a, j, b, leg], frecv.at[a, j, b], (target, z))
-
-        via_y = (chip == owner) | ((x_chip == owner) & (b < n_seq // 2))
-        via_x = (chip == owner) | ((y_chip == owner) & (b >= n_seq // 2))
+        return remote(block, block, fsend.at[a, j, b, leg], frecv.at[a, j, b], (target, z))
+
+    def from_source(a, i):
+        b = order(i)
         return (
-            (mine & via_x, to(2 * x_chip + core, 0)),
-            (mine & via_y, to(2 * y_chip + core, 1)),
-            (mine, to(sibling, 2)),
+            pass_on(a, slot, b, 2 * x_chip + core, 0),
+            pass_on(a, slot, b, 2 * y_chip + core, 1),
+            pass_on(a, slot, b, sibling, 2),
         )
 
+    is_source = home == z
+    relays = core == src_core
+
+    def relayed(a, i, j):
+        b = order(i)
+        if i % 2 == 0:
+            return relays & (x_chip == chips[j]), pass_on(a, j, b, 2 * y_chip + core, 1)
+        return relays & (y_chip == chips[j]), pass_on(a, j, b, 2 * x_chip + core, 0)
+
+    def shared(a, i, j):
+        return relays & (chip != chips[j]), pass_on(a, j, order(i), sibling, 2)
+
     for a in range(2):
-        for b in range(n_seq):
+
+        @pl.when(is_source)
+        def _():
+            for i in range(n_seq):
+                if i == 0:
+                    own_copy(a).wait()
+                else:
+                    pass_on(a, slot, order(i), me, 0).wait_recv()
+                for copy in from_source(a, i):
+                    copy.start()
+
+    for a in range(2):
+        for i in range(n_seq):
             for j in range(2):
-                block = outs[a].at[j, b]
-                held = (me == 2 * chips[j] + src_core) & (z == b)
-
-                @pl.when(held)
+
+                @pl.when(jnp.logical_not(is_source & (slot == j)))
                 def _():
-                    own_copy(a).wait()
-
-                @pl.when(jnp.logical_not(held))
-                def _():
-                    remote(block, block, zsend.at[a], frecv.at[a, j, b], (me, z)).wait_recv()
-
-                for use, copy in forwards(a, j, b):
+                    pass_on(a, j, order(i), me, 0).wait_recv()
+
+                for use, copy in (relayed(a, i, j), shared(a, i, j)):
 
                     @pl.when(use)
                     def _():
@@ -374,16 +371,14 @@
 
     for step in range(1, n_dp):
         peer = lax.rem(me + step, n_dp)
-        for group in range(4):
-            w_arrive(peer, group).wait_recv()
-            w_send(peer, group).wait_send()
+        w_arrive(peer).wait_recv()
+        w_send(peer).wait_send()
 
         @pl.when(home == z)
         def _():
             m_send(peer).wait_send()
 
-    for group in range(4):
-        w_own(group).wait()
+    w_own().wait()
 
     @pl.when(home == z)
     def _():
@@ -401,9 +396,15 @@
         def _():
             z_send(a, z).wait_send()
 
-        for b in range(n_seq):
+        @pl.when(is_source)
+        def _():
+            for i in range(n_seq):
+                for copy in from_source(a, i):
+                    copy.wait_send()
+
+        for i in range(n_seq):
             for j in range(2):
-                for use, copy in forwards(a, j, b):
+                for use, copy in (relayed(a, i, j), shared(a, i, j)):
 
                     @pl.when(use)
                     def _():
@@ -624,6 +625,7 @@
     seq_len = stamps.shape[1]
     head = lax.axis_index("dp")
     meta = jnp.concatenate([stamps.reshape(-1, DH), jnp.broadcast_to(lengths[:, None], (4, DH))])
+    w_cols = w_qkvu.reshape(-1, 4, n_dp, DH).transpose(2, 0, 1, 3).reshape(n_dp, -1, 4 * DH)
     dma = pltpu.SemaphoreType.DMA
     sds = jax.ShapeDtypeStruct
     side = pltpu.CompilerParams(has_side_effects=True)
@@ -632,7 +634,7 @@
         out_shape=(
             sds((2, n_seq, tok, width), BF16),
             sds((2, n_seq, tok, width), BF16),
-            sds((width, 4 * DH), BF16),
+            sds((n_dp, w_qkvu.shape[0], 4 * DH), BF16),
             sds((2,) + meta.shape, jnp.int32),
         ),
         in_specs=[VM] * 4,
@@ -641,15 +643,16 @@
             dma((2,)),
             dma((2, 2, n_seq, 3)),
             dma((2, 2, n_seq)),
-            dma((n_dp, 4)),
-            dma((n_dp, 4)),
+            dma((n_dp,)),
+            dma((n_dp,)),
             dma((n_dp,)),
             dma((2,)),
-            dma((7,)),
+            dma((4,)),
         ],
         compiler_params=side,
         name="gather",
-    )(tokens[0], cotangent[0], w_qkvu, meta)
+    )(tokens[0], cotangent[0], w_cols, meta)
+    w_head = w_head.reshape(width, 4 * DH)
     count = 2 * seq_len
     x_rows = x_all.reshape(count, width)
     c_rows = c_all.reshape(count, width)

time: 303 us -> 167 us (0.55)
  Pallas kernels: 268 us -> 130 us
    pallas_call x1, Pallas kernels: 195 us -> 57 us  [head_parallel(): pl.pallas_call(lambda *refs: gather_kernel(n_dp, n_seq, *refs), out_shape...]
where the time goes in v2:
time: 167 us
  Pallas kernels  130 us (78%)
  other arithmetic  17.8 us (11%)
  matrix products  10.4 us (6%)
  local copies, waits for them, and re-layouts  7 us (4%)
    pallas_call x1, Pallas kernels, head_parallel(): pl.pallas_call(lambda *refs: gather_kernel(n_dp, n_seq, *refs), out_shape...  57 us
    pallas_call x1, Pallas kernels, head_parallel(): pl.pallas_call(lambda *refs: reduce_kernel(n_dp, n_seq, *refs), out_shape...  55.6 us
    pallas_call x1, Pallas kernels, head_parallel(): pl.pallas_call(lambda *refs: stats_kernel(n_dp, *refs), out_shape=sds((n_...  6.95 us
    pallas_call x1, Pallas kernels, head_parallel(): pl.pallas_call(backward_kernel, grid=(2,), out_shape=sds((2, seq_len, 4 *...  5.23 us
    pallas_call x1, Pallas kernels, head_parallel(): pl.pallas_call(forward_kernel, grid=(2,), out_shape=(sds((2, seq_len, DH)...  5.02 us
    dot_general x1, matrix products, head_parallel(): lax.dot_general(c_rows, w_out, (((1,), (1,)), ((), ())), preferred_elemen...  3.41 us

profile of v2, /device:TPU:3, one launch (start us, length us, event | category | flops | bytes accessed | tf_op | source)
XLA Modules:
  0.0 166.6 jit_solution(16697271205894573922)
XLA Ops:
  0.6 1.5 copy.24
  2.2 0.4 copy.27
  2.6 1.2 reshape.216.refs_2_
  4.5 0.6 concatenate.4.refs_3_
  5.1 57.0 %gather.1 = (bf16[2,4,128,1024]{3,2,1,0:T(8,128)(2,1)}, bf16[2,4,128,1024]{3,2,1,0:T(8,128)(2,1)}, bf16[8,128,512]{2,1,0:T(8,128)(2,1)}, s32[2,8,128]{2,1,0:T(8,128)}) custom-call(bf16[128,1024]{1,0:T(8,128)(2,1)} %bitcast.108, bf16[128,1024]{1,0:T(8,128)(2,1)} %bitcast.119, bf16[8,128,512]{2,1,0:T(8,128)(2,1)} %reshape.216.refs_2_, s32[8,128]{1,0:T(8,128)} %concatenate.4.refs_3_), custom_call_target="tpu_custom_call" | custom-call | tf_op jit(solution)/shard_map/gather/pallas_call | solution.py:632
  62.1 2.1 %convert_reduce_fusion = f32[2,4,128]{2,1,0:T(4,128)S(1)} fusion(bf16[2,4,128,1024]{3,2,1,0:T(8,128)(2,1)} %get-tuple-element.13), kind=kLoop, calls=%fused_computation.1 | loop fusion | flops 2096128 | bytes 2101248 | tf_op jit(solution)/shard_map/reduce_sum | solution.py:16
  64.3 0.7 fusion.2
  65.1 0.7 fusion.4
  65.8 0.5 copy-done.12
  66.3 2.6 %fusion.31 = f32[1024,512]{1,0:T(8,128)} fusion(bf16[1024,1024]{1,0:T(8,128)(2,1)S(1)} %bitcast.113, bf16[1024,512]{1,0:T(8,128)(2,1)S(1)} %bitcast.125), kind=kOutput, calls=%fused_computation.72 | convolution fusion | flops 1073741824 | bytes 5242880 | tf_op jit(solution)/shard_map/dot_general | solution.py:663
  68.9 1.1 reshape_reshape.4.scol_ref
  70.0 0.6 slice_reduce_fusion.len_ref
  70.7 5.0 %forward.1 = (f32[2,512,128]{2,1,0:T(8,128)}, bf16[2,512,512]{2,1,0:T(8,128)(2,1)}, f32[2,512,512]{2,1,0:T(8,128)}) custom-call(f32[8,16]{1,0:T(8,128)} %bias_ref.1, s32[2]{0:T(128)} %slice_reduce_fusion.len_ref, f32[2,512,512]{2,1,0:T(8,128)} %bitcast.105, s32[2,1,512]{2,1,0:T(1,128)} %bitcast.120, s32[2,512,1]{2,1,0:T(8,128)} %reshape_reshape.4.scol_ref), custom_call_target="tpu_custom_call" | custom-call | tf_op jit(solution)/shard_map/forward/pallas_call | solution.py:670
  75.7 1.3 reduce_sum.138
  77.0 0.8 dynamic_slice.3
  77.8 3.4 %fusion.30 = (f32[1024]{0:T(1024)S(1)}, f32[1024]{0:T(1024)S(1)}, f32[1024,128]{1,0:T(8,128)}, f32[1024,128]{1,0:T(8,128)}) fusion(f32[1024]{0:T(1024)S(1)} %bitcast.121, f32[2,512,128]{2,1,0:T(8,128)} %get-tuple-element.15, f32[128]{0:T(128)S(1)} %dynamic_slice.3, f32[1024,512]{1,0:T(8,128)S(1)} %copy-done.2, bf16[1024,1024]{1,0:T(8,128)(2,1)} %bitcast.111, ...), kind=kOutput, calls=%fused_computation.71 | convolution fusion | flops 269744128 | bytes 4469248 | tf_op jit(solution)/shard_map/dot_general | solution.py:685
  81.2 0.4 multiply_reduce_fusion
  81.6 0.6 pad_maximum_fusion.1.refs_0_
  82.2 7.0 %stats.1 = f32[8,4,8,128]{3,2,1,0:T(8,128)} custom-call(f32[4,8,128]{2,1,0:T(8,128)} %pad_maximum_fusion.1.refs_0_), custom_call_target="tpu_custom_call" | custom-call | tf_op jit(solution)/shard_map/stats/pallas_call | solution.py:692
  89.2 0.8 bitcast_reduce_fusion
  90.0 0.8 fusion.23
  90.8 2.6 %multiply_convert_fusion.1 = (bf16[1024,128]{1,0:T(8,128)(2,1)S(1)}, f32[1024,128]{1,0:T(8,128)}, bf16[1024,128]{1,0:T(8,128)(2,1)}) fusion(f32[2,512,128]{2,1,0:T(8,128)S(1)} %copy-done.4, f32[1024]{0:T(1024)S(1)} %get-tuple-element.43, f32[1024]{0:T(1024)S(1)} %get-tuple-element.35, f32[128]{0:T(128)S(1)} %dynamic_slice.3, f32[1024,512]{1,0:T(8,128)S(1)} %copy-done.2, ...), kind=kLoop, calls=%fused_computation.40 | loop fusion | flops 1966080 | bytes 3162624 | tf_op jit(solution)/shard_map/convert_element_type | solution.py:711
  93.5 5.2 %backward.1 = bf16[2,512,512]{2,1,0:T(8,128)(2,1)} custom-call(f32[2,512,512]{2,1,0:T(8,128)} %bitcast.106, bf16[2,512,128]{2,1,0:T(8,128)(2,1)} %bitcast.116, f32[2,512,128]{2,1,0:T(8,128)} %bitcast.114, bf16[2,512,512]{2,1,0:T(8,128)(2,1)} %get-tuple-element.17.weight_ref, f32[2,512,512]{2,1,0:T(8,128)} %get-tuple-element.18.slope_ref), custom_call_target="tpu_custom_call" | custom-call | tf_op jit(solution)/shard_map/backward/pallas_call | solution.py:714
  98.7 2.5 %convolution_convert_fusion = bf16[1024,1024]{1,0:T(8,128)(2,1)S(1)} fusion(bf16[1024,512]{1,0:T(8,128)(2,1)} %bitcast.117, bf16[1024,512]{1,0:T(8,128)(2,1)S(1)} %bitcast.126), kind=kOutput, calls=%fused_computation.8 | convolution fusion | flops 1074790400 | bytes 4194304 | tf_op jit(solution)/shard_map/dot_general | solution.py:730
  101.2 0.7 convolution_convert_fusion.1
  101.9 2.3 %pad_maximum_fusion.refs_0_ = bf16[2,8,128,1024]{3,2,1,0:T(8,128)(2,1)} fusion(bf16[1,8,128,1024]{3,2,1,0:T(8,128)(2,1)S(1)} %bitcast.115, bf16[1,8,128,1024]{3,2,1,0:T(8,128)(2,1)S(1)} %bitcast.107), kind=kLoop, calls=%fused_computation.7 | loop fusion | flops 2097152 | bytes 8388608 | tf_op jit(solution)/shard_map/stack | solution.py:764
  104.2 1.2 convolution_convert_fusion.2.refs_1_
  105.4 55.6 %reduce.9 = (bf16[2,128,1024]{2,1,0:T(8,128)(2,1)}, bf16[128,1024]{1,0:T(8,128)(2,1)}) custom-call(bf16[2,8,128,1024]{3,2,1,0:T(8,128)(2,1)} %pad_maximum_fusion.refs_0_, bf16[128,1024]{1,0:T(8,128)(2,1)} %convolution_convert_fusion.2.refs_1_), custom_call_target="tpu_custom_call" | custom-call | tf_op jit(solution)/shard_map/reduce/pallas_call | solution.py:738
  161.2 1.2 fusion.13
  162.4 1.2 fusion.18
  163.7 2.0 %fusion.17 = (bf16[1,128,1024]{2,1,0:T(8,128)(2,1)}, bf16[1,128,1024]{2,1,0:T(8,128)(2,1)}) fusion(bf16[1,128,1024]{2,1,0:T(8,128)(2,1)S(1)} %copy-done.3, bf16[1,128,1024]{2,1,0:T(8,128)(2,1)S(1)} %copy-done.6, f32[128]{0:T(128)S(1)} %negate_multiply_fusion, f32[128]{0:T(128)S(1)} %get-tuple-element.40, f32[128]{0:T(128)S(1)} %broadcast_multiply_fusion.3, ...), kind=kLoop, calls=%fused_computation.32 | loop fusion | flops 1966080 | bytes 1579008 | tf_op jit(solution)/shard_map/convert_element_type | solution.py:769
  165.7 0.8 convert_element_type.79
  (41 shorter events, 0.4 us)
Async XLA Ops:
  0.6 77.1 %copy-start = (bf16[128,1024]{1,0:T(8,128)(2,1)S(1)}, bf16[128,1024]{1,0:T(8,128)(2,1)}, u32[]{:S(2)}) copy-start(bf16[128,1024]{1,0:T(8,128)(2,1)} %param.14) | copy-start | bytes 786436
  2.1 2.3 %copy-start.11 = (s32[1,512]{1,0:T(1,128)S(1)}, s32[1,512]{1,0:T(1,128)}, u32[]{:S(2)}) copy-start(s32[1,512]{1,0:T(1,128)} %param.11) | copy-start | bytes 6148
  62.1 2.2 %copy-start.1 = (bf16[2,4,128,1024]{3,2,1,0:T(8,128)(2,1)S(1)}, bf16[2,4,128,1024]{3,2,1,0:T(8,128)(2,1)}, u32[]{:S(2)}) copy-start(bf16[2,4,128,1024]{3,2,1,0:T(8,128)(2,1)} %get-tuple-element.13) | copy-start | bytes 6291460
  62.1 2.9 %copy-start.8 = (f32[1024]{0:T(1024)S(1)}, f32[1024]{0:T(1024)}, u32[]{:S(2)}) copy-start(f32[1024]{0:T(1024)} %param.15) | copy-start | bytes 12292
  65.1 1.2 copy-start.12
  66.3 2.6 %copy-start.10 = (s32[2,8,128]{2,1,0:T(8,128)S(1)}, s32[2,8,128]{2,1,0:T(8,128)}, u32[]{:S(2)}) copy-start(s32[2,8,128]{2,1,0:T(8,128)} %get-tuple-element.12) | copy-start | bytes 24580
  68.9 8.9 %copy-start.2 = (f32[1024,512]{1,0:T(8,128)S(1)}, f32[1024,512]{1,0:T(8,128)}, u32[]{:S(2)}) copy-start(f32[1024,512]{1,0:T(8,128)} %fusion.31) | copy-start | bytes 6291460
  68.9 1.8 %copy-start.9 = (s32[2,4,128]{2,1,0:T(4,128)}, s32[2,4,128]{2,1,0:T(4,128)S(1)}, u32[]{:S(2)}) copy-start(s32[2,4,128]{2,1,0:T(4,128)S(1)} %slice.28) | copy-start | bytes 12292
  77.8 3.4 %copy-start.4 = (f32[2,512,128]{2,1,0:T(8,128)S(1)}, f32[2,512,128]{2,1,0:T(8,128)}, u32[]{:S(2)}) copy-start(f32[2,512,128]{2,1,0:T(8,128)} %get-tuple-element.15) | copy-start | bytes 1572868
  93.5 5.2 %copy-start.13 = (bf16[8,128,512]{2,1,0:T(8,128)(2,1)S(1)}, bf16[8,128,512]{2,1,0:T(8,128)(2,1)}, u32[]{:S(2)}) copy-start(bf16[8,128,512]{2,1,0:T(8,128)(2,1)} %get-tuple-element.14) | copy-start | bytes 3145732
  101.9 2.3 %copy-start.5 = (bf16[2,4,128,1024]{3,2,1,0:T(8,128)(2,1)S(1)}, bf16[2,4,128,1024]{3,2,1,0:T(8,128)(2,1)}, u32[]{:S(2)}) copy-start(bf16[2,4,128,1024]{3,2,1,0:T(8,128)(2,1)} %get-tuple-element.16) | copy-start | bytes 6291460
  105.4 55.7 %copy-start.3 = (bf16[1,128,1024]{2,1,0:T(8,128)(2,1)S(1)}, bf16[1,128,1024]{2,1,0:T(8,128)(2,1)}, u32[]{:S(2)}) copy-start(bf16[1,128,1024]{2,1,0:T(8,128)(2,1)} %param.9) | copy-start | bytes 786436
  105.4 58.2 %copy-start.6 = (bf16[1,128,1024]{2,1,0:T(8,128)(2,1)S(1)}, bf16[1,128,1024]{2,1,0:T(8,128)(2,1)}, u32[]{:S(2)}) copy-start(bf16[1,128,1024]{2,1,0:T(8,128)(2,1)} %param.10) | copy-start | bytes 786436
  161.1 4.7 %copy-start.7 = (bf16[128,1024]{1,0:T(8,128)(2,1)S(1)}, bf16[128,1024]{1,0:T(8,128)(2,1)}, u32[]{:S(2)}) copy-start(bf16[128,1024]{1,0:T(8,128)(2,1)} %get-tuple-element.20) | copy-start | bytes 786436

commit v3 on v2

--- a/solution.py
+++ b/solution.py
@@ -254,7 +254,7 @@
 
 
 def gather_kernel(
-    n_dp, n_seq, x_ref, c_ref, w_ref, m_ref, xo_ref, co_ref, wo_ref, mo_ref,
+    n_dp, n_seq, x_ref, c_ref, w_ref, m_ref, gain_ref, proj_ref, co_ref, wo_ref, mo_ref, xo_ref,
     zsend, fsend, frecv, wsend, wrecv, msend, mrecv, local_sem,
 ):
     me = lax.axis_index("dp")
@@ -355,6 +355,12 @@
                 for copy in from_source(a, i):
                     copy.start()
 
+    def project(i, j):
+        b = order(i)
+        normed = layer_norm(xo_ref[j, b].astype(F32), gain_ref[...]).astype(BF16)
+        weights = wo_ref[...].reshape(-1, 4 * DH)
+        proj_ref[j, b] = jnp.dot(normed, weights, preferred_element_type=F32)
+
     for a in range(2):
         for i in range(n_seq):
             for j in range(2):
@@ -369,16 +375,21 @@
                     def _():
                         copy.start()
 
+                if a == 1:
+                    project(i, j)
+
+        if a == 0:
+            w_own().wait()
+            for step in range(1, n_dp):
+                w_arrive(lax.rem(me + step, n_dp)).wait_recv()
+
     for step in range(1, n_dp):
         peer = lax.rem(me + step, n_dp)
-        w_arrive(peer).wait_recv()
         w_send(peer).wait_send()
 
         @pl.when(home == z)
         def _():
             m_send(peer).wait_send()
-
-    w_own().wait()
 
     @pl.when(home == z)
     def _():
@@ -414,6 +425,12 @@
 def stats_kernel(n_dp, s_ref, o_ref, send, recv, local_sem):
     me = lax.axis_index("dp")
     z = lax.axis_index("seq")
+    barrier = pltpu.get_barrier_semaphore()
+    for step in range(1, n_dp):
+        pl.semaphore_signal(
+            barrier, inc=1, device_id=(lax.rem(me + step, n_dp), z), device_id_type=MESH
+        )
+    pl.semaphore_wait(barrier, n_dp - 1)
     own = pltpu.make_async_copy(s_ref, o_ref.at[me], local_sem)
     own.start()
     for step in range(1, n_dp):
@@ -428,7 +445,7 @@
 
 
 def reduce_kernel(
-    n_dp, n_seq, p_ref, g_ref, o_ref, go_ref, pair, mixed_up, landed, final, g_land, g_sum,
+    n_dp, n_seq, pm_ref, pd_ref, g_ref, o_ref, go_ref, pair, mixed_up, landed, final, g_land, g_sum,
     psend, precv, csend, crecv, osend, orecv, gsend, grecv, hsend, hrecv, local_sem,
 ):
     me = lax.axis_index("dp")
@@ -437,13 +454,14 @@
     sibling = 2 * chip + (1 - core)
     chips_n = n_dp // 2
     g_rows = g_ref.shape[0] // n_seq
+    p_refs = (pm_ref, pd_ref)
 
     def g_slice(ref, index):
         return ref.at[pl.ds(pl.multiple_of(index * g_rows, g_rows), g_rows)]
 
     def pair_send(part, c):
         return remote(
-            p_ref.at[part, 2 * c + (1 - core)], pair.at[part, c],
+            p_refs[part].at[2 * c + (1 - core)], pair.at[part, c],
             psend.at[part, c], precv.at[part, c], (sibling, z),
         )
 
@@ -477,7 +495,7 @@
 
     others = [lax.rem(chip + step, chips_n) for step in range(1, chips_n)]
     peers = [lax.rem(z + step, n_seq) for step in range(1, n_seq)]
-    parts = p_ref.shape[0]
+    parts = len(p_refs)
     for part in range(parts):
         for c in others + [chip]:
             pair_send(part, c).start()
@@ -487,7 +505,7 @@
         for c in others + [chip]:
             pair_send(part, c).wait_recv()
             mixed_up[part, c] = (
-                p_ref[part, 2 * c + core].astype(F32) + pair[part, c].astype(F32)
+                p_refs[part][2 * c + core].astype(F32) + pair[part, c].astype(F32)
             ).astype(BF16)
             if c is not chip:
                 cross_send(part, c).start()
@@ -629,17 +647,18 @@
     dma = pltpu.SemaphoreType.DMA
     sds = jax.ShapeDtypeStruct
     side = pltpu.CompilerParams(has_side_effects=True)
-    x_all, c_all, w_head, metas = pl.pallas_call(
+    projected, c_all, w_head, metas = pl.pallas_call(
         lambda *refs: gather_kernel(n_dp, n_seq, *refs),
         out_shape=(
-            sds((2, n_seq, tok, width), BF16),
+            sds((2, n_seq, tok, 4 * DH), F32),
             sds((2, n_seq, tok, width), BF16),
             sds((n_dp, w_qkvu.shape[0], 4 * DH), BF16),
             sds((2,) + meta.shape, jnp.int32),
         ),
-        in_specs=[VM] * 4,
+        in_specs=[VM] * 5,
         out_specs=[VM] * 4,
         scratch_shapes=[
+            pltpu.VMEM((2, n_seq, tok, width), BF16),
             dma((2,)),
             dma((2, 2, n_seq, 3)),
             dma((2, 2, n_seq)),
@@ -651,16 +670,14 @@
         ],
         compiler_params=side,
         name="gather",
-    )(tokens[0], cotangent[0], w_cols, meta)
+    )(tokens[0], cotangent[0], w_cols, meta, gain_in[None])
     w_head = w_head.reshape(width, 4 * DH)
     count = 2 * seq_len
-    x_rows = x_all.reshape(count, width)
     c_rows = c_all.reshape(count, width)
     stamp_rows = metas[:, : seq_len // DH].reshape(2, 1, seq_len)
     stamp_cols = stamp_rows.reshape(2, seq_len, 1)
     spans = metas[:, seq_len // DH, 0]
-    normed = layer_norm(x_rows.astype(F32), gain_in).astype(BF16)
-    projected = jnp.dot(normed, w_head, preferred_element_type=F32)
+    projected = projected.reshape(count, 4 * DH)
     proj3 = projected.reshape(2, seq_len, 4 * DH)
     smem = pl.BlockSpec(memory_space=pltpu.SMEM)
 
@@ -695,7 +712,7 @@
         in_specs=[VM],
         out_specs=VM,
         scratch_shapes=[dma((n_dp,)), dma((n_dp,)), dma],
-        compiler_params=side,
+        compiler_params=pltpu.CompilerParams(has_side_effects=True, collective_id=1),
         name="stats",
     )(stats.reshape(4, count // DH, DH))
     means, squares, g_sums, g_offs = [gathered[:, k] for k in range(4)]
@@ -738,7 +755,7 @@
     sums, w_sum = pl.pallas_call(
         lambda *refs: reduce_kernel(n_dp, n_seq, *refs),
         out_shape=(sds((2, tok, width), BF16), sds(w_part.shape, BF16)),
-        in_specs=[VM] * 2,
+        in_specs=[VM] * 3,
         out_specs=[VM] * 2,
         scratch_shapes=[
             pltpu.VMEM((2, half, tok, width), BF16),
@@ -761,7 +778,7 @@
         ],
         compiler_params=side,
         name="reduce",
-    )(jnp.stack([mixed_part.reshape(shape), d_part.reshape(shape)]), w_part)
+    )(mixed_part.reshape(shape), d_part.reshape(shape), w_part)
     wide_rows = tokens[0].astype(F32)
     mixed = (wide_rows + sums[0].astype(F32)).astype(BF16)
     unused_rows, in_back = jax.vjp(lambda values: layer_norm(values, gain_in), wide_rows)

time: 167 us -> 160 us (0.958)
  other arithmetic: 17.8 us -> 12.1 us
  Pallas kernels: 130 us -> 127 us
    convert_element_type x2 -> x0, other arithmetic: 3.33 us -> none  [the longest x1 2.64 us: head_parallel(): mixed_rows = (normed_att * gate).astype(BF16)]
    pallas_call x1, Pallas kernels: 55.6 us -> 52.8 us  [head_parallel(): pl.pallas_call(lambda *refs: reduce_kernel(n_dp, n_seq, *refs), out_shape...]
    mul x0 -> x1, other arithmetic: none -> 2.63 us  [head_parallel(): d_gate = d_mix * normed_att]
    dot_general x1 -> x0, matrix products: 2.6 us -> none  [head_parallel(): projected = jnp.dot(normed, w_head, preferred_element_type=F32)]
    another operation x1 -> x0, other arithmetic: 2.29 us -> none  [head_parallel(): jnp.stack([mixed_part.reshape(shape), d_part.reshape(shape)])]
    reduce_sum x2 -> x1, other arithmetic: 2.2 us -> 0.12 us  [layer_norm(): average = jnp.mean(values, axis=-1, keepdims=True)]
where the time goes in v3:
time: 160 us; the launch traced here: 159 us
  Pallas kernels  127 us (79%)
  other arithmetic  12.1 us (8%)
  matrix products  10.4 us (6%)
  local copies, waits for them, and re-layouts  7.9 us (5%)
    pallas_call x1, Pallas kernels, head_parallel(): pl.pallas_call(lambda *refs: gather_kernel(n_dp, n_seq, *refs), out_shape...  58 us
    pallas_call x1, Pallas kernels, head_parallel(): pl.pallas_call(lambda *refs: reduce_kernel(n_dp, n_seq, *refs), out_shape...  52.8 us
    pallas_call x1, Pallas kernels, head_parallel(): pl.pallas_call(lambda *refs: stats_kernel(n_dp, *refs), out_shape=sds((n_...  6.38 us
    pallas_call x1, Pallas kernels, head_parallel(): pl.pallas_call(backward_kernel, grid=(2,), out_shape=sds((2, seq_len, 4 *...  5.17 us
    pallas_call x1, Pallas kernels, head_parallel(): pl.pallas_call(forward_kernel, grid=(2,), out_shape=(sds((2, seq_len, DH)...  5.07 us
    dot_general x1, matrix products, head_parallel(): lax.dot_general(d_proj.reshape(count, 4 * DH), w_head, (((1,), (1,)), (()...  3.86 us
    dot_general x1, matrix products, head_parallel(): lax.dot_general(c_rows, w_out, (((1,), (1,)), ((), ())), preferred_elemen...  3.41 us

profile of v3, /device:TPU:3, one launch (start us, length us, event | category | flops | bytes accessed | tf_op | source)
XLA Modules:
  0.0 159.4 jit_solution(13988979423373660119)
XLA Ops:
  0.6 0.0 copy-start
  0.6 1.5 copy.24
  2.1 0.0 copy-start.9
  2.2 0.4 copy.27
  2.6 1.2 reshape.183.refs_2_
  4.5 0.6 concatenate.4.refs_3_
  5.1 58.0 %gather.1 = (f32[2,4,128,512]{3,2,1,0:T(8,128)}, bf16[2,4,128,1024]{3,2,1,0:T(8,128)(2,1)}, bf16[8,128,512]{2,1,0:T(8,128)(2,1)}, s32[2,8,128]{2,1,0:T(8,128)}) custom-call(bf16[128,1024]{1,0:T(8,128)(2,1)} %bitcast.109, bf16[128,1024]{1,0:T(8,128)(2,1)} %bitcast.119, bf16[8,128,512]{2,1,0:T(8,128)(2,1)} %reshape.183.refs_2_, s32[8,128]{1,0:T(8,128)} %concatenate.4.refs_3_, ...), custom_call_target="tpu_custom_call" | custom-call | tf_op jit(solution)/shard_map/gather/pallas_call | solution.py:650
  63.1 0.8 slice.28
  64.0 1.1 reshape_reshape.8.scol_ref
  65.1 1.3 slice_reduce_fusion.len_ref
  66.4 0.0 copy-done.8
  66.4 5.1 %forward.1 = (f32[2,512,128]{2,1,0:T(8,128)}, bf16[2,512,512]{2,1,0:T(8,128)(2,1)}, f32[2,512,512]{2,1,0:T(8,128)}) custom-call(f32[8,16]{1,0:T(8,128)} %bias_ref.1, s32[2]{0:T(128)} %slice_reduce_fusion.len_ref, f32[2,512,512]{2,1,0:T(8,128)} %bitcast.104, s32[2,1,512]{2,1,0:T(1,128)} %bitcast.121, s32[2,512,1]{2,1,0:T(8,128)} %reshape_reshape.8.scol_ref), custom_call_target="tpu_custom_call" | custom-call | tf_op jit(solution)/shard_map/forward/pallas_call | solution.py:687
  71.5 1.3 reduce_sum.118
  72.8 0.8 dynamic_slice.3
  73.6 0.0 copy-done
  73.6 3.4 %fusion.25 = (f32[1024]{0:T(1024)S(1)}, f32[1024]{0:T(1024)S(1)}, f32[1024,128]{1,0:T(8,128)}, f32[1024,128]{1,0:T(8,128)}) fusion(f32[1024]{0:T(1024)S(1)} %bitcast.122, f32[2,512,128]{2,1,0:T(8,128)} %get-tuple-element.14, f32[128]{0:T(128)S(1)} %dynamic_slice.3, f32[1024,512]{1,0:T(8,128)S(1)} %bitcast.106, bf16[1024,1024]{1,0:T(8,128)(2,1)} %bitcast.112, ...), kind=kOutput, calls=%fused_computation.61 | convolution fusion | flops 269744128 | bytes 4469248 | tf_op jit(solution)/shard_map/dot_general | solution.py:702
  77.0 0.4 multiply_reduce_fusion
  77.4 0.6 pad_maximum_fusion.refs_0_
  78.0 6.4 %stats.1 = f32[8,4,8,128]{3,2,1,0:T(8,128)} custom-call(f32[4,8,128]{2,1,0:T(8,128)} %pad_maximum_fusion.refs_0_), custom_call_target="tpu_custom_call" | custom-call | tf_op jit(solution)/shard_map/stats/pallas_call | solution.py:709
  84.4 0.9 bitcast_reduce_fusion
  85.3 0.8 fusion.20
  86.2 2.6 %multiply_multiply_fusion.1 = (f32[1024,128]{1,0:T(8,128)}, bf16[1024,128]{1,0:T(8,128)(2,1)S(1)}, bf16[1024,128]{1,0:T(8,128)(2,1)}) fusion(f32[1024,128]{1,0:T(8,128)} %get-tuple-element.41, f32[2,512,128]{2,1,0:T(8,128)S(1)} %copy-done.3, f32[1024]{0:T(1024)S(1)} %get-tuple-element.43, f32[1024]{0:T(1024)S(1)} %get-tuple-element.35, ...), kind=kLoop, calls=%fused_computation.36 | loop fusion | flops 1966080 | bytes 3162624 | tf_op jit(solution)/shard_map/mul | solution.py:729
  88.8 1.2 convolution_convert_fusion.2.refs_2_
  90.0 5.2 %backward.1 = bf16[2,512,512]{2,1,0:T(8,128)(2,1)} custom-call(f32[2,512,512]{2,1,0:T(8,128)} %bitcast.105, bf16[2,512,128]{2,1,0:T(8,128)(2,1)} %bitcast.116, f32[2,512,128]{2,1,0:T(8,128)} %bitcast.115, bf16[2,512,512]{2,1,0:T(8,128)(2,1)} %get-tuple-element.16.weight_ref, f32[2,512,512]{2,1,0:T(8,128)} %get-tuple-element.17.slope_ref), custom_call_target="tpu_custom_call" | custom-call | tf_op jit(solution)/shard_map/backward/pallas_call | solution.py:731
  95.2 3.9 %convolution_convert_fusion = bf16[1024,1024]{1,0:T(8,128)(2,1)} fusion(bf16[1024,512]{1,0:T(8,128)(2,1)} %bitcast.117, bf16[1024,512]{1,0:T(8,128)(2,1)S(1)} %bitcast.126), kind=kOutput, calls=%fused_computation | convolution fusion | flops 1074790400 | bytes 4194304 | tf_op jit(solution)/shard_map/dot_general | solution.py:747
  99.0 2.0 %convolution_convert_fusion.1 = bf16[1024,1024]{1,0:T(8,128)(2,1)} fusion(bf16[1024,128]{1,0:T(8,128)(2,1)S(1)} %get-tuple-element.33, bf16[128,1024]{1,0:T(8,128)(2,1)S(1)} %copy-done), kind=kOutput, calls=%fused_computation.1 | convolution fusion | flops 269484032 | bytes 2621440 | tf_op jit(solution)/shard_map/dot_general | solution.py:746
  101.0 52.8 %reduce.7 = (bf16[2,128,1024]{2,1,0:T(8,128)(2,1)}, bf16[128,1024]{1,0:T(8,128)(2,1)}) custom-call(bf16[8,128,1024]{2,1,0:T(8,128)(2,1)} %bitcast.108, bf16[8,128,1024]{2,1,0:T(8,128)(2,1)} %bitcast.114, bf16[128,1024]{1,0:T(8,128)(2,1)} %convolution_convert_fusion.2.refs_2_), custom_call_target="tpu_custom_call" | custom-call | tf_op jit(solution)/shard_map/reduce/pallas_call | solution.py:755
  153.9 0.1 convert_reduce_fusion
  154.0 1.2 fusion.8
  155.2 1.2 fusion.13
  156.5 2.0 %fusion.12 = (bf16[1,128,1024]{2,1,0:T(8,128)(2,1)}, bf16[1,128,1024]{2,1,0:T(8,128)(2,1)}) fusion(bf16[1,128,1024]{2,1,0:T(8,128)(2,1)S(1)} %copy-done.2, bf16[1,128,1024]{2,1,0:T(8,128)(2,1)S(1)} %copy-done.5, f32[128]{0:T(128)S(1)} %negate_multiply_fusion, f32[128]{0:T(128)S(1)} %get-tuple-element.40, f32[128]{0:T(128)S(1)} %broadcast_multiply_fusion.2, ...), kind=kLoop, calls=%fused_computation.24 | loop fusion | flops 1966080 | bytes 1579008 | tf_op jit(solution)/shard_map/convert_element_type | solution.py:786
  158.5 0.8 convert_element_type.64
  (28 shorter events, 0.1 us)
Async XLA Ops:
  0.6 72.9 %copy-start = (bf16[128,1024]{1,0:T(8,128)(2,1)S(1)}, bf16[128,1024]{1,0:T(8,128)(2,1)}, u32[]{:S(2)}) copy-start(bf16[128,1024]{1,0:T(8,128)(2,1)} %param.14) | copy-start | bytes 786436
  2.1 2.3 %copy-start.9 = (s32[1,512]{1,0:T(1,128)S(1)}, s32[1,512]{1,0:T(1,128)}, u32[]{:S(2)}) copy-start(s32[1,512]{1,0:T(1,128)} %param.11) | copy-start | bytes 6148
  63.1 10.5 %copy-start.1 = (f32[2,4,128,512]{3,2,1,0:T(8,128)S(1)}, f32[2,4,128,512]{3,2,1,0:T(8,128)}, u32[]{:S(2)}) copy-start(f32[2,4,128,512]{3,2,1,0:T(8,128)} %get-tuple-element.13) | copy-start | bytes 6291460
  63.9 2.5 %copy-start.8 = (s32[2,4,128]{2,1,0:T(4,128)}, s32[2,4,128]{2,1,0:T(4,128)S(1)}, u32[]{:S(2)}) copy-start(s32[2,4,128]{2,1,0:T(4,128)S(1)} %slice.28) | copy-start | bytes 12292
  73.6 3.4 %copy-start.3 = (f32[2,512,128]{2,1,0:T(8,128)S(1)}, f32[2,512,128]{2,1,0:T(8,128)}, u32[]{:S(2)}) copy-start(f32[2,512,128]{2,1,0:T(8,128)} %get-tuple-element.14) | copy-start | bytes 1572868
  84.4 4.5 %copy-start.4 = (bf16[2,4,128,1024]{3,2,1,0:T(8,128)(2,1)S(1)}, bf16[2,4,128,1024]{3,2,1,0:T(8,128)(2,1)}, u32[]{:S(2)}) copy-start(bf16[2,4,128,1024]{3,2,1,0:T(8,128)(2,1)} %get-tuple-element.15) | copy-start | bytes 6291460
  90.0 5.2 %copy-start.10 = (bf16[8,128,512]{2,1,0:T(8,128)(2,1)S(1)}, bf16[8,128,512]{2,1,0:T(8,128)(2,1)}, u32[]{:S(2)}) copy-start(bf16[8,128,512]{2,1,0:T(8,128)(2,1)} %get-tuple-element.18) | copy-start | bytes 3145732
  101.0 52.9 %copy-start.2 = (bf16[1,128,1024]{2,1,0:T(8,128)(2,1)S(1)}, bf16[1,128,1024]{2,1,0:T(8,128)(2,1)}, u32[]{:S(2)}) copy-start(bf16[1,128,1024]{2,1,0:T(8,128)(2,1)} %param.9) | copy-start | bytes 786436
  101.0 53.0 %copy-start.7 = (f32[1024]{0:T(1024)S(1)}, f32[1024]{0:T(1024)}, u32[]{:S(2)}) copy-start(f32[1024]{0:T(1024)} %param.15) | copy-start | bytes 12292
  101.0 55.5 %copy-start.5 = (bf16[1,128,1024]{2,1,0:T(8,128)(2,1)S(1)}, bf16[1,128,1024]{2,1,0:T(8,128)(2,1)}, u32[]{:S(2)}) copy-start(bf16[1,128,1024]{2,1,0:T(8,128)(2,1)} %param.10) | copy-start | bytes 786436
  153.9 4.7 %copy-start.6 = (bf16[128,1024]{1,0:T(8,128)(2,1)S(1)}, bf16[128,1024]{1,0:T(8,128)(2,1)}, u32[]{:S(2)}) copy-start(bf16[128,1024]{1,0:T(8,128)(2,1)} %get-tuple-element.20) | copy-start | bytes 786436
